TPU v7x, 512 devices: a whole 4x8x8 slice. The times are simulated.
512 devices in a mesh: seq: 128 (over z, x, y_lo, core), head: 4 (over y_hi).
Axes of the slice: x: 4, y: 8 (y_hi: 4, y_lo: 2; y = y_hi * 2 + y_lo), z: 8, core: 2. Of those that a mesh axis runs over, the one named last changes fastest.
Arguments:
- query: bfloat16 [2, 16384, 4096], P(None, 'seq', 'head'), may hold values from -5 to 5
- keys: bfloat16 [2, 16384, 1024], P(None, 'seq', 'head'), may hold values from -5 to 5
- values: bfloat16 [2, 16384, 1024], P(None, 'seq', 'head'), may hold values from -12 to 12
- norm_gain: float32 [4096], P('head'), may hold values from 0.25 to 1.75
- in_b: bfloat16 [32768, 128], P('seq'), may hold values from -0.25 to 0.25
- out_c: bfloat16 [32768, 128], P('seq'), may hold values from -0.25 to 0.25
- step: float32 [64, 32768], P('head', 'seq'), may hold values from 0.2 to 1
- log_decay: float32 [64, 32768], P('head', 'seq'), may hold values from -2 to 0
- skip: float32 [64], P('head'), may hold values from 0.5 to 1.5
Outputs:
- mixed: bfloat16 [32768, 4096], P('seq', 'head')
All inputs are finite; a program needn't handle non-finite values.
Results may differ from a plain program's by a relative error of at most 0.012.
Values may be sent and summed in bfloat16 or wider, within the bound.
A program may use at most 128 MiB of HBM per device.

v0:
```python
import math

import jax
import jax.numpy as jnp
from jax import lax
from jax.sharding import Mesh
from jax.sharding import PartitionSpec as P

HEADS = 32
HDIM = 128
SDIM = 64
STATE = 128
SPAN = 256
SEQ = ("seq_0", "seq_1", "seq_2", "seq_3")


def from_behind(block, axis, distance):
    devices = range(lax.axis_size(axis))
    route = [((i - distance) % len(devices), i) for i in devices]
    return lax.ppermute(block, axis, route)


def partner(block, axis, stride):
    count = lax.axis_size(axis)
    route = []
    for low in range(count):
        high = low | 1 << stride
        if high != low and high < count:
            route += [(low, high), (high, low)]
    return lax.ppermute(block, axis, route)


def copy_for_each(value, axis):
    copies = jnp.broadcast_to(value, (lax.axis_size(axis), *value.shape))
    return lax.all_to_all(copies, axis, split_axis=0, concat_axis=0, tiled=True)


def over_copies(value, axis):
    everything = copy_for_each(value, axis)
    return jnp.sum(everything, axis=0)


def filled_with(value, identity):
    return jax.tree.map(
        lambda part, zero: jnp.zeros_like(part) + jnp.asarray(zero, part.dtype), value, identity
    )


def prefix_by_axis(value, axes, combine, identity):
    before = start = filled_with(value, identity)
    running = value
    for axis in reversed(axes):
        count, here = (lax.axis_size(axis), lax.axis_index(axis))
        pieces = jax.tree.map(
            lambda part, kind: lax.all_gather(part.astype(kind), axis),
            running,
            (jnp.bfloat16, jnp.bfloat16),
        )
        inside, running = (start, start)
        for k in range(count):
            passed = k < here
            running = combine(
                running, jax.tree.map(lambda part, own: part[k].astype(own.dtype), pieces, value)
            )
            inside = jax.tree.map(lambda new, old: jnp.where(passed, new, old), running, inside)
        before = combine(inside, before)
    return before


def combine_states(earlier, later):
    return (earlier[0] + later[0], jnp.exp(later[0])[:, None, None] * earlier[1] + later[1])


def body(query, keys, values, norm_gain, in_b, out_c, step, log_decay, skip):
    seq_count = lax.axis_size(SEQ)
    seq_index = lax.axis_index(SEQ)
    blk_rows = query.shape[1]
    feat_local = query.shape[2]
    kv_local = keys.shape[2] // HDIM
    group_size = feat_local // HDIM // kv_local
    score_scale = 1.0 / math.sqrt(HDIM)
    near_kv = from_behind((keys, values), SEQ, 1)
    far_kv = from_behind((keys, values), SEQ, 2)
    near_kv = tuple((jnp.where(seq_index == 0, member[::-1], member) for member in near_kv))
    far_kv = tuple((jnp.where(seq_index < 2, member[::-1], member) for member in far_kv))
    outputs = []
    for slot_id in range(2):
        block_id = seq_index + seq_count * slot_id
        key_rows = jnp.concatenate([far_kv[0][slot_id], near_kv[0][slot_id], keys[slot_id]], 0)
        val_rows = jnp.concatenate([far_kv[1][slot_id], near_kv[1][slot_id], values[slot_id]], 0)
        query_heads = query[slot_id].reshape(blk_rows, kv_local, group_size, HDIM)
        key_heads = key_rows.reshape(3 * blk_rows, kv_local, HDIM)
        val_heads = val_rows.reshape(3 * blk_rows, kv_local, HDIM)
        scores = (
            jnp.einsum("qgjd,kgd->gjqk", query_heads, key_heads, preferred_element_type=jnp.float32)
            * score_scale
        )
        query_pos = block_id * blk_rows + jnp.arange(blk_rows, dtype=jnp.int32)
        key_pos = (block_id - 2) * blk_rows + jnp.arange(3 * blk_rows, dtype=jnp.int32)
        window = 2 * blk_rows
        allowed = (
            (key_pos[None, :] <= query_pos[:, None])
            & (key_pos[None, :] > query_pos[:, None] - window)
            & (key_pos[None, :] >= 0)
        )
        scores = jnp.where(allowed, scores, -jnp.inf)
        row_peak = jnp.max(scores, axis=-1, keepdims=True)
        exp_terms = jnp.exp(scores - row_peak)
        row_total = jnp.sum(exp_terms, axis=-1)
        weights = exp_terms.astype(jnp.bfloat16)
        result = jnp.einsum(
            "gjqk,kgd->qgjd", weights, val_heads, preferred_element_type=jnp.float32
        )
        result = result / jnp.transpose(row_total, (2, 0, 1))[..., None]
        outputs.append(result.reshape(blk_rows, feat_local).astype(jnp.bfloat16))
    lead_slot = outputs[0]
    tail_slot = outputs[1]
    for bit_pos in reversed(range(seq_count.bit_length() - 1)):
        upper_half = jnp.right_shift(seq_index, bit_pos) % 2 == 1
        outgoing = jnp.where(upper_half, lead_slot, tail_slot)
        incoming = partner(outgoing, SEQ, bit_pos)
        lead_slot = jnp.where(upper_half, incoming, lead_slot)
        tail_slot = jnp.where(upper_half, tail_slot, incoming)
    attended = jnp.concatenate([lead_slot, tail_slot], 0)
    widened = attended.astype(jnp.float32)
    row_sums = over_copies(jnp.sum(widened * widened, axis=-1), "head")
    meansq = row_sums / (HEADS * HDIM)
    normed = (widened * norm_gain[None, :] * lax.rsqrt(meansq + 1e-06)[:, None]).astype(
        jnp.bfloat16
    )
    highest = lax.Precision.HIGHEST
    tok_rows = normed.shape[0]
    heads_ssm = step.shape[0]
    span_count = tok_rows // SPAN
    inputs_low = normed.reshape(span_count, SPAN, heads_ssm, SDIM)
    inputs = inputs_low.astype(jnp.float32)
    in_low = in_b.reshape(span_count, SPAN, STATE)
    out_low = out_c.reshape(span_count, SPAN, STATE)
    in_rows = in_low.astype(jnp.float32)
    out_rows = out_low.astype(jnp.float32)
    step_rows = step.reshape(heads_ssm, span_count, SPAN).transpose(1, 0, 2)
    decay_rows = log_decay.reshape(heads_ssm, span_count, SPAN).transpose(1, 0, 2)
    cum_log = jnp.cumsum(decay_rows, axis=2)
    causal = jnp.arange(SPAN)[:, None] >= jnp.arange(SPAN)[None, :]
    decay_mat = jnp.exp(
        jnp.where(causal[None, None], cum_log[:, :, :, None] - cum_log[:, :, None, :], -jnp.inf)
    )
    cross_terms = jnp.einsum("ctn,cun->ctu", out_low, in_low, preferred_element_type=jnp.float32)
    mixing = (decay_mat * cross_terms[:, None] * step_rows[:, :, None, :]).astype(jnp.bfloat16)
    local_out = jnp.einsum(
        "chtu,cuhe->cthe", mixing, inputs_low, preferred_element_type=jnp.float32
    )
    span_totals = cum_log[:, :, -1]
    end_weights = jnp.exp(span_totals[:, :, None] - cum_log) * step_rows
    weighted = end_weights.transpose(0, 2, 1)[..., None] * inputs
    span_states = jnp.einsum("cuhe,cun->chen", weighted, in_rows, precision=highest)
    incl_log = jnp.cumsum(span_totals, axis=0)
    excl_log = incl_log - span_totals
    dev_total = incl_log[-1]
    dev_state = jnp.einsum(
        "ch,chen->hen", jnp.exp(dev_total[None, :] - incl_log), span_states, precision=highest
    )
    earlier_mask = jnp.arange(span_count)[:, None] > jnp.arange(span_count)[None, :]
    pair_weights = jnp.exp(
        jnp.where(earlier_mask[:, :, None], excl_log[:, None, :] - incl_log[None, :, :], -jnp.inf)
    )
    local_start = jnp.einsum("kjh,jhen->khen", pair_weights, span_states, precision=highest)
    entry_scale = jnp.exp(cum_log).transpose(0, 2, 1)[..., None]
    identity = (
        jnp.zeros((heads_ssm,), jnp.float32),
        jnp.zeros((heads_ssm, SDIM, STATE), jnp.float32),
    )
    entering = prefix_by_axis((dev_total, dev_state), SEQ, combine_states, identity)[1]
    starts = local_start + jnp.exp(excl_log)[:, :, None, None] * entering[None]
    entry_term = jnp.einsum("ctn,chen->cthe", out_rows, starts, precision=highest) * entry_scale
    result = local_out + entry_term
    result = result + skip[None, None, :, None] * inputs
    return result.reshape(tok_rows, heads_ssm * SDIM).astype(jnp.bfloat16)


def solution(mesh):
    torus = Mesh(
        mesh.devices.reshape(8, 4, 2, 2, mesh.shape["head"]),
        ("seq_0", "seq_1", "seq_2", "seq_3", "head"),
    )
    return jax.shard_map(
        body,
        mesh=torus,
        in_specs=(
            P(None, SEQ, "head"),
            P(None, SEQ, "head"),
            P(None, SEQ, "head"),
            P("head"),
            P(SEQ, None),
            P(SEQ, None),
            P("head", SEQ),
            P("head", SEQ),
            P("head"),
        ),
        out_specs=P(SEQ, "head"),
        check_vma=False,
    )
```

profile of v0, /device:TPU:1, one launch (start us, length us, event | category | flops | bytes accessed | tf_op | source)
XLA Modules:
  0.0 220.1 jit_solution(108554590417269829)
XLA Ops:
  6.5 1.1 copy.155
  7.6 4.0 %collective-permute-start.2 = (bf16[2,128,256]{1,2,0:T(8,128)(2,1)S(1)}, bf16[2,128,256]{1,2,0:T(8,128)(2,1)S(1)}, u32[]{:S(2)}, u32[]{:S(2)}) collective-permute-start(bf16[2,128,256]{1,2,0:T(8,128)(2,1)S(1)} %copy.155), channel_id=1, source_target_pairs={{504,0},{508,4},{0,8},{4,12},{8,16},{12,20},{16,24},{20,28},{24,32... | collective-permute-start | bytes 393224 | tf_op jit(solution)/shard_map/ppermute | solution.py:20
  11.7 3.8 %collective-permute-start.3 = (bf16[2,128,256]{1,2,0:T(8,128)(2,1)S(1)}, bf16[2,128,256]{1,2,0:T(8,128)(2,1)S(1)}, u32[]{:S(2)}, u32[]{:S(2)}) collective-permute-start(bf16[2,128,256]{1,2,0:T(8,128)(2,1)S(1)} %copy.155), channel_id=1, source_target_pairs={{508,0},{0,4},{4,8},{8,12},{12,16},{16,20},{20,24},{24,28},{28,32}... | collective-permute-start | bytes 393224 | tf_op jit(solution)/shard_map/ppermute | solution.py:20
  15.5 1.0 copy.152
  16.5 3.2 %collective-permute-start = (bf16[2,128,256]{1,2,0:T(8,128)(2,1)S(1)}, bf16[2,128,256]{1,2,0:T(8,128)(2,1)S(1)}, u32[]{:S(2)}, u32[]{:S(2)}) collective-permute-start(bf16[2,128,256]{1,2,0:T(8,128)(2,1)S(1)} %copy.152), channel_id=1, source_target_pairs={{504,0},{508,4},{0,8},{4,12},{8,16},{12,20},{16,24},{20,28},{24,32... | collective-permute-start | bytes 393224 | tf_op jit(solution)/shard_map/ppermute | solution.py:20
  19.8 2.2 collective-permute-start.1
  22.0 0.9 fusion.195
  24.3 1.3 collective-permute-done.2
  25.9 4.5 %collective-permute-done = bf16[2,128,256]{1,2,0:T(8,128)(2,1)S(1)} collective-permute-done((bf16[2,128,256]{1,2,0:T(8,128)(2,1)S(1)}, bf16[2,128,256]{1,2,0:T(8,128)(2,1)S(1)}, u32[]{:S(2)}, u32[]{:S(2)}) %collective-permute-start) | collective-permute-done | bytes 131104 | tf_op jit(solution)/shard_map/ppermute | solution.py:20
  30.8 0.4 fusion.200
  31.2 0.2 fusion.7
  31.4 0.4 fusion.199
  31.8 0.2 fusion.9
  32.0 0.4 fusion.19
  32.4 0.4 fusion.20
  32.9 7.6 %collective-permute-start.4 = (bf16[128,1024]{0,1:T(8,128)(2,1)S(1)}, bf16[128,1024]{0,1:T(8,128)(2,1)S(1)}, u32[]{:S(2)}, u32[]{:S(2)}) collective-permute-start(bf16[128,1024]{0,1:T(8,128)(2,1)S(1)} %bitcast_select_fusion.3), channel_id=1, source_target_pairs={{0,256},{256,0},{4,260},{260,4},{8,264},{264,8},{12,268},{268,12},... | collective-permute-start | bytes 786440 | tf_op jit(solution)/shard_map/ppermute | solution.py:30
  40.5 4.1 %collective-permute-done.4 = bf16[128,1024]{0,1:T(8,128)(2,1)S(1)} collective-permute-done((bf16[128,1024]{0,1:T(8,128)(2,1)S(1)}, bf16[128,1024]{0,1:T(8,128)(2,1)S(1)}, u32[]{:S(2)}, u32[]{:S(2)}) %collective-permute-start.4) | collective-permute-done | bytes 262176 | tf_op jit(solution)/shard_map/ppermute | solution.py:30
  44.7 9.9 %collective-permute-start.5 = (bf16[128,1024]{0,1:T(8,128)(2,1)S(1)}, bf16[128,1024]{0,1:T(8,128)(2,1)S(1)}, u32[]{:S(2)}, u32[]{:S(2)}) collective-permute-start(bf16[128,1024]{0,1:T(8,128)(2,1)S(1)} %get-tuple-element.14), channel_id=1, source_target_pairs={{0,128},{128,0},{4,132},{132,4},{8,136},{136,8},{12,140},{140,12},... | collective-permute-start | bytes 786440 | tf_op jit(solution)/shard_map/ppermute | solution.py:30
  54.6 9.8 %collective-permute-done.5 = bf16[128,1024]{0,1:T(8,128)(2,1)S(1)} collective-permute-done((bf16[128,1024]{0,1:T(8,128)(2,1)S(1)}, bf16[128,1024]{0,1:T(8,128)(2,1)S(1)}, u32[]{:S(2)}, u32[]{:S(2)}) %collective-permute-start.5) | collective-permute-done | bytes 262176 | tf_op jit(solution)/shard_map/ppermute | solution.py:30
  64.4 1.9 collective-permute-start.6
  66.4 6.4 %collective-permute-done.6 = bf16[128,1024]{0,1:T(8,128)(2,1)S(1)} collective-permute-done((bf16[128,1024]{0,1:T(8,128)(2,1)S(1)}, bf16[128,1024]{0,1:T(8,128)(2,1)S(1)}, u32[]{:S(2)}, u32[]{:S(2)}) %collective-permute-start.6) | collective-permute-done | bytes 262176 | tf_op jit(solution)/shard_map/ppermute | solution.py:30
  72.8 3.6 %collective-permute-start.7 = (bf16[128,1024]{0,1:T(8,128)(2,1)S(1)}, bf16[128,1024]{0,1:T(8,128)(2,1)S(1)}, u32[]{:S(2)}, u32[]{:S(2)}) collective-permute-start(bf16[128,1024]{0,1:T(8,128)(2,1)S(1)} %get-tuple-element.11), channel_id=1, source_target_pairs={{0,32},{32,0},{4,36},{36,4},{8,40},{40,8},{12,44},{44,12},{16,48},... | collective-permute-start | bytes 786440 | tf_op jit(solution)/shard_map/ppermute | solution.py:30
  76.5 0.6 reduce-window.6
  77.1 4.8 %collective-permute-done.7 = bf16[128,1024]{0,1:T(8,128)(2,1)S(1)} collective-permute-done((bf16[128,1024]{0,1:T(8,128)(2,1)S(1)}, bf16[128,1024]{0,1:T(8,128)(2,1)S(1)}, u32[]{:S(2)}, u32[]{:S(2)}) %collective-permute-start.7) | collective-permute-done | bytes 262176 | tf_op jit(solution)/shard_map/ppermute | solution.py:30
  81.9 7.0 %collective-permute-start.8 = (bf16[128,1024]{0,1:T(8,128)(2,1)S(1)}, bf16[128,1024]{0,1:T(8,128)(2,1)S(1)}, u32[]{:S(2)}, u32[]{:S(2)}) collective-permute-start(bf16[128,1024]{0,1:T(8,128)(2,1)S(1)} %broadcast_select_fusion.11), channel_id=1, source_target_pairs={{0,16},{16,0},{4,20},{20,4},{8,24},{24,8},{12,28},{28,12},{32,48},... | collective-permute-start | bytes 786440 | tf_op jit(solution)/shard_map/ppermute | solution.py:30
  89.3 4.1 %collective-permute-done.8 = bf16[128,1024]{0,1:T(8,128)(2,1)S(1)} collective-permute-done((bf16[128,1024]{0,1:T(8,128)(2,1)S(1)}, bf16[128,1024]{0,1:T(8,128)(2,1)S(1)}, u32[]{:S(2)}, u32[]{:S(2)}) %collective-permute-start.8) | collective-permute-done | bytes 262176 | tf_op jit(solution)/shard_map/ppermute | solution.py:30
  93.4 1.9 collective-permute-start.9
  95.4 5.1 %all-gather = bf16[2,16,1]{1,2,0:T(2,128)(2,1)S(1)} all-gather(bf16[1,16,1]{1,2,0:T(2,128)(2,1)S(1)} %slice.444), channel_id=2, replica_groups=mesh['seq_0'=8,'seq_1'=4,'seq_2'=2,'seq_3'=2,'head'=4] {'seq_3'}, dimensions={0}, use_global_device_ids=true | all-gather | bytes 96 | tf_op jit(solution)/shard_map/all_gather | solution.py:55
  100.6 5.8 %collective-permute-start.10 = (bf16[128,1024]{0,1:T(8,128)(2,1)S(1)}, bf16[128,1024]{0,1:T(8,128)(2,1)S(1)}, u32[]{:S(2)}, u32[]{:S(2)}) collective-permute-start(bf16[128,1024]{0,1:T(8,128)(2,1)S(1)} %broadcast_select_fusion.17), channel_id=1, source_target_pairs={{0,4},{4,0},{8,12},{12,8},{16,20},{20,16},{24,28},{28,24},{32,36},... | collective-permute-start | bytes 786440 | tf_op jit(solution)/shard_map/ppermute | solution.py:30
  106.4 3.1 %all-gather.2 = bf16[2,1,16]{2,1,0:T(2,128)(2,1)S(1)} all-gather(bf16[1,1,16]{2,1,0:T(2,128)(2,1)S(1)} %get-tuple-element.51), channel_id=1, replica_groups=mesh['seq_0'=8,'seq_1'=4,'seq_2'=2,'seq_3'=2,'head'=4] {'seq_2'}, dimensions={0}, use_global_device_ids=true | all-gather | bytes 96 | tf_op jit(solution)/shard_map/all_gather | solution.py:55
  109.8 0.2 multiply_reduce_fusion
  110.0 0.6 broadcast_in_dim.35
  110.6 5.8 %all-to-all-start = ((f32[4,1,256]{2,1,0:T(1,128)}), f32[4,1,256]{2,1,0:T(1,128)S(1)}, u32[]{:S(2)}, u32[]{:S(2)}) async-start(f32[4,1,256]{2,1,0:T(1,128)} %broadcast_in_dim.35), calls=%async_computation | async-start | bytes 8192 | tf_op jit(solution)/shard_map/all_to_all | solution.py:35
  116.4 6.5 %all-to-all-done = f32[4,1,256]{2,1,0:T(1,128)S(1)} async-done(((f32[4,1,256]{2,1,0:T(1,128)}), f32[4,1,256]{2,1,0:T(1,128)S(1)}, u32[]{:S(2)}, u32[]{:S(2)}) %all-to-all-start) | async-done | bytes 4128 | tf_op jit(solution)/shard_map/all_to_all | solution.py:35
  122.9 0.8 multiply_convert_fusion.12
  123.7 4.2 %all-gather.1 = bf16[32,64,128]{2,1,0:T(8,128)(2,1)S(1)} all-gather(bf16[16,64,128]{2,1,0:T(8,128)(2,1)S(1)} %get-tuple-element.60), channel_id=3, replica_groups=mesh['seq_0'=8,'seq_1'=4,'seq_2'=2,'seq_3'=2,'head'=4] {'seq_3'}, dimensions={0}, use_global_device_ids=true | all-gather | bytes 786432 | tf_op jit(solution)/shard_map/all_gather | solution.py:55
  127.9 0.2 fusion.68
  128.1 8.7 %all_gather.40 = bf16[2,16,64,128]{3,2,1,0:T(8,128)(2,1)S(1)} all-gather(bf16[1,16,64,128]{3,2,1,0:T(8,128)(2,1)S(1)} %fusion.68), channel_id=1, replica_groups=mesh['seq_0'=8,'seq_1'=4,'seq_2'=2,'seq_3'=2,'head'=4] {'seq_2'}, dimensions={0}, use_global_device_ids=true | all-gather | bytes 786432 | tf_op jit(solution)/shard_map/all_gather | solution.py:55
  136.8 1.0 fusion.46
  137.9 7.6 %all-gather.3 = bf16[4,1,16]{2,1,0:T(2,128)(2,1)S(1)} all-gather(bf16[1,1,16]{2,1,0:T(2,128)(2,1)S(1)} %get-tuple-element.54), channel_id=1, replica_groups=mesh['seq_0'=8,'seq_1'=4,'seq_2'=2,'seq_3'=2,'head'=4] {'seq_1'}, dimensions={0}, use_global_device_ids=true | all-gather | bytes 160 | tf_op jit(solution)/shard_map/all_gather | solution.py:55
  145.5 16.9 %all-gather.8.cloned.1.call-done = bf16[4,16,64,128]{3,2,1,0:T(8,128)(2,1)} async-done(((bf16[1,16,64,128]{3,2,1,0:T(8,128)(2,1)}), bf16[4,16,64,128]{3,2,1,0:T(8,128)(2,1)}) %all-gather.8.cloned.1.call-update) | async-done | bytes 1048592 | tf_op jit(solution)/shard_map/all_gather | solution.py:55
  162.4 2.2 %fusion.62 = bf16[1,16,64,128]{3,2,1,0:T(8,128)(2,1)} fusion(f32[16]{0:T(128)S(1)} %get-tuple-element.49, f32[16]{0:T(128)S(1)} %get-tuple-element.48, f32[16]{0:T(128)S(1)} %get-tuple-element.47, f32[16]{0:T(128)S(1)} %get-tuple-element.46, bf16[4,16,64,128]{3,2,1,0:T(8,128)(2,1)} %all-gather.8.cloned.1.call-done), kind=kLoop, calls=%fused_computation.82 | loop fusion | flops 1572864 | bytes 1310976 | tf_op jit(solution)/shard_map/convert_element_type | solution.py:55
  164.8 13.5 %all-gather.4 = bf16[8,1,16]{2,1,0:T(2,128)(2,1)S(1)} all-gather(bf16[1,1,16]{2,1,0:T(2,128)(2,1)S(1)} %get-tuple-element.45), channel_id=1, replica_groups=mesh['seq_0'=8,'seq_1'=4,'seq_2'=2,'seq_3'=2,'head'=4] {'seq_0'}, dimensions={0}, use_global_device_ids=true | all-gather | bytes 288 | tf_op jit(solution)/shard_map/all_gather | solution.py:55
  178.3 0.2 fusion.201
  178.5 28.6 %all-gather.10.cloned.1.call-done = bf16[8,16,64,128]{3,2,1,0:T(8,128)(2,1)} async-done(((bf16[1,16,64,128]{3,2,1,0:T(8,128)(2,1)}), bf16[8,16,64,128]{3,2,1,0:T(8,128)(2,1)}) %all-gather.10.cloned.1.call-update) | async-done | bytes 2097168 | tf_op jit(solution)/shard_map/all_gather | solution.py:55
  207.1 3.6 %fusion.13 = f32[1,256,16,64]{1,3,2,0:T(8,128)S(1)} fusion(f32[256,16]{0,1:T(8,128)S(1)} %copy.178, f32[16,64,128]{2,1,0:T(8,128)S(1)} %get-tuple-element.61, bf16[8,16,64,128]{3,2,1,0:T(8,128)(2,1)} %all-gather.10.cloned.1.call-done, f32[16]{0:T(128)S(1)} %get-tuple-element.52, f32[16]{0:T(128)S(1)} %get-tuple-element.50, f32[16]{0:T(128)S(1)} %get-tuple-element.55, ...), kind=kOutput, calls=%fused_computation.19 | convolution fusion | flops 411959296 | bytes 5850384 | tf_op jit(solution)/shard_map/ctn,chen->cthe/dot_general | solution.py:175
  210.7 1.6 fusion.16
  212.3 1.0 copy.179
  (85 shorter events, 3.4 us)
Async XLA Ops:
  6.5 116.4 %copy-start = (bf16[256,128]{1,0:T(8,128)(2,1)S(1)}, bf16[256,128]{1,0:T(8,128)(2,1)}, u32[]{:S(2)}) copy-start(bf16[256,128]{1,0:T(8,128)(2,1)} %param.13) | copy-start | bytes 196612
  6.5 16.6 %copy-start.1 = (bf16[2,128,1024]{2,1,0:T(8,128)(2,1)S(1)}, bf16[2,128,1024]{2,1,0:T(8,128)(2,1)}, u32[]{:S(2)}) copy-start(bf16[2,128,1024]{2,1,0:T(8,128)(2,1)} %param.9) | copy-start | bytes 1572868
  7.6 17.9 %collective-permute-start.2 = (bf16[2,128,256]{1,2,0:T(8,128)(2,1)S(1)}, bf16[2,128,256]{1,2,0:T(8,128)(2,1)S(1)}, u32[]{:S(2)}, u32[]{:S(2)}) collective-permute-start(bf16[2,128,256]{1,2,0:T(8,128)(2,1)S(1)} %copy.155), channel_id=1, source_target_pairs={{504,0},{508,4},{0,8},{4,12},{8,16},{12,20},{16,24},{20,28},{24,32... | collective-permute-start | bytes 393224 | tf_op jit(solution)/shard_map/ppermute | solution.py:20
  11.7 14.0 %collective-permute-start.3 = (bf16[2,128,256]{1,2,0:T(8,128)(2,1)S(1)}, bf16[2,128,256]{1,2,0:T(8,128)(2,1)S(1)}, u32[]{:S(2)}, u32[]{:S(2)}) collective-permute-start(bf16[2,128,256]{1,2,0:T(8,128)(2,1)S(1)} %copy.155), channel_id=1, source_target_pairs={{508,0},{0,4},{4,8},{8,12},{12,16},{16,20},{20,24},{24,28},{28,32}... | collective-permute-start | bytes 393224 | tf_op jit(solution)/shard_map/ppermute | solution.py:20
  16.5 13.9 %collective-permute-start = (bf16[2,128,256]{1,2,0:T(8,128)(2,1)S(1)}, bf16[2,128,256]{1,2,0:T(8,128)(2,1)S(1)}, u32[]{:S(2)}, u32[]{:S(2)}) collective-permute-start(bf16[2,128,256]{1,2,0:T(8,128)(2,1)S(1)} %copy.152), channel_id=1, source_target_pairs={{504,0},{508,4},{0,8},{4,12},{8,16},{12,20},{16,24},{20,28},{24,32... | collective-permute-start | bytes 393224 | tf_op jit(solution)/shard_map/ppermute | solution.py:20
  19.8 10.7 %collective-permute-start.1 = (bf16[2,128,256]{1,2,0:T(8,128)(2,1)S(1)}, bf16[2,128,256]{1,2,0:T(8,128)(2,1)S(1)}, u32[]{:S(2)}, u32[]{:S(2)}) collective-permute-start(bf16[2,128,256]{1,2,0:T(8,128)(2,1)S(1)} %copy.152), channel_id=1, source_target_pairs={{508,0},{0,4},{4,8},{8,12},{12,16},{16,20},{20,24},{24,28},{28,32}... | collective-permute-start | bytes 393224 | tf_op jit(solution)/shard_map/ppermute | solution.py:20
  32.9 11.7 %collective-permute-start.4 = (bf16[128,1024]{0,1:T(8,128)(2,1)S(1)}, bf16[128,1024]{0,1:T(8,128)(2,1)S(1)}, u32[]{:S(2)}, u32[]{:S(2)}) collective-permute-start(bf16[128,1024]{0,1:T(8,128)(2,1)S(1)} %bitcast_select_fusion.3), channel_id=1, source_target_pairs={{0,256},{256,0},{4,260},{260,4},{8,264},{264,8},{12,268},{268,12},... | collective-permute-start | bytes 786440 | tf_op jit(solution)/shard_map/ppermute | solution.py:30
  44.7 31.7 %copy-start.4 = (f32[16,256]{1,0:T(8,128)S(1)}, f32[16,256]{1,0:T(8,128)}, u32[]{:S(2)}) copy-start(f32[16,256]{1,0:T(8,128)} %param.16) | copy-start | bytes 49156
  44.7 19.6 %collective-permute-start.5 = (bf16[128,1024]{0,1:T(8,128)(2,1)S(1)}, bf16[128,1024]{0,1:T(8,128)(2,1)S(1)}, u32[]{:S(2)}, u32[]{:S(2)}) collective-permute-start(bf16[128,1024]{0,1:T(8,128)(2,1)S(1)} %get-tuple-element.14), channel_id=1, source_target_pairs={{0,128},{128,0},{4,132},{132,4},{8,136},{136,8},{12,140},{140,12},... | collective-permute-start | bytes 786440 | tf_op jit(solution)/shard_map/ppermute | solution.py:30
  64.4 8.4 %collective-permute-start.6 = (bf16[128,1024]{0,1:T(8,128)(2,1)S(1)}, bf16[128,1024]{0,1:T(8,128)(2,1)S(1)}, u32[]{:S(2)}, u32[]{:S(2)}) collective-permute-start(bf16[128,1024]{0,1:T(8,128)(2,1)S(1)} %broadcast_select_fusion.5), channel_id=1, source_target_pairs={{0,64},{64,0},{4,68},{68,4},{8,72},{72,8},{12,76},{76,12},{16,80},... | collective-permute-start | bytes 786440 | tf_op jit(solution)/shard_map/ppermute | solution.py:30
  72.8 9.0 %collective-permute-start.7 = (bf16[128,1024]{0,1:T(8,128)(2,1)S(1)}, bf16[128,1024]{0,1:T(8,128)(2,1)S(1)}, u32[]{:S(2)}, u32[]{:S(2)}) collective-permute-start(bf16[128,1024]{0,1:T(8,128)(2,1)S(1)} %get-tuple-element.11), channel_id=1, source_target_pairs={{0,32},{32,0},{4,36},{36,4},{8,40},{40,8},{12,44},{44,12},{16,48},... | collective-permute-start | bytes 786440 | tf_op jit(solution)/shard_map/ppermute | solution.py:30
  81.9 11.5 %collective-permute-start.8 = (bf16[128,1024]{0,1:T(8,128)(2,1)S(1)}, bf16[128,1024]{0,1:T(8,128)(2,1)S(1)}, u32[]{:S(2)}, u32[]{:S(2)}) collective-permute-start(bf16[128,1024]{0,1:T(8,128)(2,1)S(1)} %broadcast_select_fusion.11), channel_id=1, source_target_pairs={{0,16},{16,0},{4,20},{20,4},{8,24},{24,8},{12,28},{28,12},{32,48},... | collective-permute-start | bytes 786440 | tf_op jit(solution)/shard_map/ppermute | solution.py:30
  89.2 20.4 %copy-start.3 = (f32[16,256]{1,0:T(8,128)S(1)}, f32[16,256]{1,0:T(8,128)}, u32[]{:S(2)}) copy-start(f32[16,256]{1,0:T(8,128)} %param.15) | copy-start | bytes 49156
  93.4 7.1 %collective-permute-start.9 = (bf16[128,1024]{0,1:T(8,128)(2,1)S(1)}, bf16[128,1024]{0,1:T(8,128)(2,1)S(1)}, u32[]{:S(2)}, u32[]{:S(2)}) collective-permute-start(bf16[128,1024]{0,1:T(8,128)(2,1)S(1)} %get-tuple-element.8), channel_id=1, source_target_pairs={{0,8},{8,0},{4,12},{12,4},{16,24},{24,16},{20,28},{28,20},{32,40},... | collective-permute-start | bytes 786440 | tf_op jit(solution)/shard_map/ppermute | solution.py:30
  100.6 15.8 %copy-start.5 = (f32[1024]{0:T(1024)S(1)}, f32[1024]{0:T(1024)}, u32[]{:S(2)}) copy-start(f32[1024]{0:T(1024)} %param.12) | copy-start | bytes 12292
  100.6 9.1 %collective-permute-start.10 = (bf16[128,1024]{0,1:T(8,128)(2,1)S(1)}, bf16[128,1024]{0,1:T(8,128)(2,1)S(1)}, u32[]{:S(2)}, u32[]{:S(2)}) collective-permute-start(bf16[128,1024]{0,1:T(8,128)(2,1)S(1)} %broadcast_select_fusion.17), channel_id=1, source_target_pairs={{0,4},{4,0},{8,12},{12,8},{16,20},{20,16},{24,28},{28,24},{32,36},... | collective-permute-start | bytes 786440 | tf_op jit(solution)/shard_map/ppermute | solution.py:30
  110.6 12.3 %all-to-all-start = ((f32[4,1,256]{2,1,0:T(1,128)}), f32[4,1,256]{2,1,0:T(1,128)S(1)}, u32[]{:S(2)}, u32[]{:S(2)}) async-start(f32[4,1,256]{2,1,0:T(1,128)} %broadcast_in_dim.35), calls=%async_computation | async-start | bytes 8192 | tf_op jit(solution)/shard_map/all_to_all | solution.py:35
  116.3 46.1 %all-gather.8.cloned.1.call-start = ((), (), s32[]{:S(2)}) async-start(), calls=%async_computation.1 | async-start | bytes 1310720 | tf_op jit(solution)/shard_map/all_gather | solution.py:55
  136.8 41.5 %copy-start.2 = (bf16[256,128]{1,0:T(8,128)(2,1)S(1)}, bf16[256,128]{1,0:T(8,128)(2,1)}, u32[]{:S(2)}) copy-start(bf16[256,128]{1,0:T(8,128)(2,1)} %param.14) | copy-start | bytes 196612
  137.8 69.3 %all-gather.10.cloned.1.call-start = ((), (), s32[]{:S(2)}) async-start(), calls=%async_computation.2 | async-start | bytes 2359296 | tf_op jit(solution)/shard_map/all_gather | solution.py:55
  207.1 3.6 %copy-start.6 = (f32[16]{0:T(128)S(1)}, f32[16]{0:T(128)}, u32[]{:S(2)}) copy-start(f32[16]{0:T(128)} %param.17) | copy-start | bytes 196
Sparse Core Ops, SparseCore 0:
  137.9 24.4 all-gather.7
  164.8 42.2 all-gather.9
where the time goes:
time: 224 us; the launch traced here: 220 us
  waiting for transfers between devices  87 us (39%)
  starting transfers between devices  56.7 us (25%)
  blocking collectives  42.1 us (19%)
  between operations  14.1 us (6%)
  matrix products  7.69 us (3%)
  local copies, waits for them, and re-layouts  6.52 us (3%)
  other arithmetic  5.95 us (3%)
    all_gather x2, waiting for transfers between devices, prefix_by_axis(): lax.all_gather(part.astype(kind), axis)  45.4 us
    all_gather x6, blocking collectives, prefix_by_axis(): lax.all_gather(part.astype(kind), axis)  42.1 us
    ppermute x7, starting transfers between devices, partner(): return lax.ppermute(block, axis, route)  37.6 us
    ppermute x7, waiting for transfers between devices, partner(): return lax.ppermute(block, axis, route)  29.3 us
    ppermute x4, starting transfers between devices, from_behind(): return lax.ppermute(block, axis, route)  13.3 us
    all_to_all x1, waiting for transfers between devices, copy_for_each(): return lax.all_to_all(copies, axis, split_axis=0, concat_axis=0, tiled=True)  6.46 us
    ppermute x4, waiting for transfers between devices, from_behind(): return lax.ppermute(block, axis, route)  5.78 us
    all_to_all x1, starting transfers between devices, copy_for_each(): return lax.all_to_all(copies, axis, split_axis=0, concat_axis=0, tiled=True)  5.76 us
  transfers between devices with their start and end apart: 14, of which 11 were waited for; matrix products, arithmetic and copies ran while one was open for 2% of the time, Pallas kernels for 0%

commit v1 on v0

v1 whole, which is shorter than its diff:
```python
import math

import jax
import jax.numpy as jnp
from jax import lax
from jax.experimental import pallas as pl
from jax.experimental.pallas import tpu as pltpu
from jax.sharding import Mesh
from jax.sharding import PartitionSpec as P

HDIM = 128
SDIM = 64
STATE = 128
SPAN = 256
BLK = 128
FEATS = 4096
NZ, NX, NY, NC, NH = 8, 4, 2, 2, 4
CHIPS = NZ * NX * NY
PLANE = NX * NY * NC
AXES = ("z", "x", "y", "core", "head")
SEQ = ("z", "x", "y", "core")
MESH = pl.DeviceIdType.MESH
F32 = jnp.float32
BF16 = jnp.bfloat16


def chip_coords(chip):
    return chip // (NX * NY), (chip // NY) % NX, chip % NY


def seq_coords(index):
    return index // PLANE, (index // (NY * NC)) % NX, (index // NC) % NY, index % NC


def dot(a, b, dims, **kw):
    return lax.dot_general(a, b, (dims, ((), ())), preferred_element_type=F32, **kw)


def kernel(
    q_hbm, k_hbm, v_hbm, gain_hbm, b_hbm, c_hbm, step_hbm, decay_hbm, skip_ref,
    out_ref,
    q_span, k_stage, v_stage, k_win, v_win, gain_v, b_v, c_v, step_v, decay_v,
    cum_v, w_v, v_v, gcol, mix, ecum, att, att_in, sq_out, sq_in, normed, weighted, local,
    tot_out, tot_in, plane_out, plane_in, st_out, st_in, pre_v, pre_log, run_out, run_in,
    en_out, en_in,
    load_sem, halo_send, halo_recv, swap_send, swap_recv, q_send, q_recv, att_send, att_recv,
    sq_send, sq_recv, tot_send, tot_recv, plane_send, plane_recv, st_send, st_recv,
    run_send, run_recv, log_send, log_recv, en_send, en_recv,
):
    z, x, y, core, hg = (lax.axis_index(a) for a in AXES)
    chip = (z * NX + x) * NY + y
    me = (x * NY + y) * NC + core
    seq = z * PLANE + me
    other = 1 - core
    partner = (z, x, y, other, hg)

    after = (chip + 1) % CHIPS
    az, ax, ay = chip_coords(after)
    wraps = (chip == CHIPS - 1).astype(jnp.int32)
    before = (chip + CHIPS - 1) % CHIPS
    bz, bx, by = chip_coords(before)

    span = core * CHIPS + chip
    fz, fx, fy, fc = seq_coords(span)
    source_chip = seq % CHIPS
    sz, sx, sy = chip_coords(source_chip)
    sc = seq // CHIPS
    stays = span == seq

    mine = pl.ds(pl.multiple_of((2 + core) * BLK, BLK), BLK)
    theirs = pl.ds(pl.multiple_of((2 + other) * BLK, BLK), BLK)
    prev_row = pl.ds(pl.multiple_of(core * BLK, BLK), BLK)
    loads = [
        (k_hbm, k_stage), (v_hbm, v_stage), (decay_hbm, decay_v), (step_hbm, step_v),
        (b_hbm, b_v), (c_hbm, c_v), (gain_hbm, gain_v),
        (k_hbm.at[core], k_win.at[mine]), (v_hbm.at[core], v_win.at[mine]),
        (q_hbm.at[core], q_span.at[core]),
    ]
    loads = [pltpu.make_async_copy(s, d, load_sem.at[i]) for i, (s, d) in enumerate(loads)]
    for copy in loads:
        copy.start()

    barrier = pltpu.get_barrier_semaphore()

    def greet(device):
        pl.semaphore_signal(barrier, inc=1, device_id=device, device_id_type=MESH)

    for c in range(NC):
        greet((bz, bx, by, c, hg))
    for r in range(1, NH):
        greet((sz, sx, sy, sc, (hg + r) % NH))

    @pl.when(jnp.logical_not(stays))
    def _():
        greet((sz, sx, sy, sc, hg))

    def plane_device(index):
        return (z, index // (NY * NC), (index // NC) % NY, index % NC, hg)

    def z_device(index):
        return (index, x, y, core, hg)

    def greet_plane(r, carry):
        greet(plane_device((me + r) % PLANE))
        return carry

    lax.fori_loop(1, PLANE, greet_plane, 0)

    def greet_z(r, carry):
        greet(z_device((z + r) % NZ))
        return carry

    lax.fori_loop(1, NZ, greet_z, 0)
    moves = jnp.logical_not(stays).astype(jnp.int32)
    pl.semaphore_wait(barrier, NC + NH - 1 + PLANE - 1 + NZ - 1 + moves)

    loads[0].wait()
    loads[1].wait()

    def cols(g, width=HDIM):
        return pl.ds(g * width, width)

    def halo(i, g, slot):
        stage, window = ((k_stage, k_win), (v_stage, v_win))[i]
        to = (az, ax, ay, jnp.where(wraps == 1, 1 - slot, slot), hg)
        return pltpu.make_async_remote_copy(
            src_ref=stage.at[slot, :, cols(g)], dst_ref=window.at[prev_row, cols(g)],
            send_sem=halo_send.at[i, g, slot], recv_sem=halo_recv.at[i, g, core],
            device_id=to, device_id_type=MESH,
        )

    def halo_arrival(i, g, block):
        window = (k_win, v_win)[i]
        return pltpu.make_async_remote_copy(
            src_ref=window.at[pl.ds(block * BLK, BLK), cols(g)],
            dst_ref=window.at[pl.ds(block * BLK, BLK), cols(g)],
            send_sem=halo_send.at[i, g, 0], recv_sem=halo_recv.at[i, g, block],
            device_id=partner, device_id_type=MESH,
        )

    def swap(i, g):
        stage, window = ((k_stage, k_win), (v_stage, v_win))[i]
        return pltpu.make_async_remote_copy(
            src_ref=stage.at[other, :, cols(g)], dst_ref=window.at[mine, cols(g)],
            send_sem=swap_send.at[i, g], recv_sem=swap_recv.at[i, g],
            device_id=partner, device_id_type=MESH,
        )

    def swap_arrival(i, g):
        window = (k_win, v_win)[i]
        return pltpu.make_async_remote_copy(
            src_ref=window.at[theirs, cols(g)], dst_ref=window.at[theirs, cols(g)],
            send_sem=swap_send.at[i, g], recv_sem=swap_recv.at[i, g],
            device_id=partner, device_id_type=MESH,
        )

    def q_swap(g):
        return pltpu.make_async_remote_copy(
            src_ref=q_hbm.at[other, :, cols(g, 512)],
            dst_ref=q_span.at[core, :, cols(g, 512)],
            send_sem=q_send.at[g], recv_sem=q_recv.at[g],
            device_id=partner, device_id_type=MESH,
        )

    def q_arrival(g):
        return pltpu.make_async_remote_copy(
            src_ref=q_span.at[other, :, cols(g, 512)],
            dst_ref=q_span.at[other, :, cols(g, 512)],
            send_sem=q_send.at[g], recv_sem=q_recv.at[g],
            device_id=partner, device_id_type=MESH,
        )

    for g in range(2):
        for i in range(2):
            for slot in range(2):
                halo(i, g, slot).start()
        q_swap(g).start()
        for i in range(2):
            swap(i, g).start()

    for copy in loads[2:]:
        copy.wait()
    row = lax.broadcasted_iota(jnp.int32, (SPAN, SPAN), 0)
    col = lax.broadcasted_iota(jnp.int32, (SPAN, SPAN), 1)
    causal = row <= col
    cum = dot(decay_v[...], causal.astype(F32), ((1,), (0,)), precision=lax.Precision.HIGHEST)
    total = cum[:, SPAN - 1:]
    tail = jnp.exp(total - cum) * step_v[...]
    shift = jnp.log(step_v[...]) - cum
    for k in range(16):
        cum_v[k] = jnp.broadcast_to(cum[k:k + 1], (8, SPAN))
        w_v[k] = jnp.broadcast_to(tail[k:k + 1], (8, SPAN))
        v_v[k] = jnp.broadcast_to(shift[k:k + 1], (8, SPAN))
        tot_out[k] = jnp.broadcast_to(total[k:k + 1], (8, 128))

    def tot_copy(k, at):
        return pltpu.make_async_remote_copy(
            src_ref=tot_out.at[k], dst_ref=tot_in.at[at],
            send_sem=tot_send.at[k], recv_sem=tot_recv.at[at],
            device_id=plane_device(k), device_id_type=MESH,
        )

    def start_tot(r, carry):
        tot_copy((me + r) % PLANE, me).start()
        return carry

    lax.fori_loop(1, PLANE, start_tot, 0)
    tot_in[me] = tot_out[me]

    cross = dot(b_v[...], c_v[...], ((1,), (1,)))

    def make_mix(k, carry):
        ct = cum_v[k, 0:1, :]
        for ub in range(2):
            line = v_v[k, 0:1, ub * BLK:(ub + 1) * BLK]
            colb = jnp.transpose(jnp.broadcast_to(line, (BLK, BLK)))
            arg = ct + jnp.concatenate([colb, colb], 1)
            rows = slice(ub * BLK, (ub + 1) * BLK)
            arg = jnp.where(causal[rows], arg, -jnp.inf)
            mix[k, rows] = (jnp.exp(arg) * cross[rows]).astype(BF16)
        return carry

    lax.fori_loop(0, 16, make_mix, 0)

    def make_ecum(p, carry):
        lanes = pl.ds(pl.multiple_of(p * BLK, BLK), BLK)
        for tb in range(2):
            part = slice(tb * BLK, (tb + 1) * BLK)
            pair = [
                jnp.broadcast_to(jnp.exp(cum_v[2 * p + h, 0:1, part]), (SDIM, BLK))
                for h in range(2)
            ]
            ecum[part, lanes] = jnp.transpose(jnp.concatenate(pair, 0))
        return carry

    lax.fori_loop(0, 8, make_ecum, 0)
    for p in range(8):
        line = jnp.broadcast_to(gain_v[p:p + 1, :], (BLK, BLK))
        gcol[p * BLK:(p + 1) * BLK, :] = jnp.transpose(line)

    def wait_tot(r, carry):
        tot_copy((me + r) % PLANE, (me + r) % PLANE).wait_recv()
        return carry

    lax.fori_loop(1, PLANE, wait_tot, 0)
    plane_log = tot_in[0]
    for i in range(1, PLANE):
        plane_log = plane_log + tot_in[i]
    plane_out[...] = plane_log
    plane_in[z] = plane_log

    def log_copy(to, at):
        return pltpu.make_async_remote_copy(
            src_ref=plane_out, dst_ref=plane_in.at[at],
            send_sem=log_send.at[to], recv_sem=log_recv.at[at],
            device_id=z_device(to), device_id_type=MESH,
        )

    def start_log(r, carry):
        log_copy((z + r) % NZ, z).start()
        return carry

    lax.fori_loop(1, NZ, start_log, 0)

    scale = math.log2(math.e) / math.sqrt(HDIM)
    j = lax.broadcasted_iota(jnp.int32, (3 * BLK, 4 * BLK), 0)
    i = lax.broadcasted_iota(jnp.int32, (3 * BLK, 4 * BLK), 1) % BLK
    first = (span == 0).astype(jnp.int32)

    def att_copy(g):
        part = pl.ds(g * 512, 512)
        return pltpu.make_async_remote_copy(
            src_ref=att.at[part], dst_ref=att_in.at[part],
            send_sem=att_send.at[g], recv_sem=att_recv.at[g],
            device_id=(fz, fx, fy, fc, hg), device_id_type=MESH,
        )

    def att_keep(g):
        part = pl.ds(g * 512, 512)
        return pltpu.make_async_copy(att.at[part], att_in.at[part], att_recv.at[g])

    sums = [jnp.zeros((1, BLK), F32) for _ in range(2)]
    for g in range(2):
        for t in range(2):
            for block in range(2):
                halo_arrival(t, g, block).wait_recv()
            swap_arrival(t, g).wait_recv()
        q_arrival(g).wait_recv()
        lanes = slice(g * HDIM, (g + 1) * HDIM)
        for a in range(2):
            keys = k_win[a * BLK:(a + 3) * BLK, lanes]
            vals = jnp.transpose(v_win[a * BLK:(a + 3) * BLK, lanes])
            heads = [q_span[a, :, (4 * g + h) * HDIM:(4 * g + h + 1) * HDIM] for h in range(4)]
            score = dot(keys, jnp.concatenate(heads, 0), ((1,), (1,)))
            low = jnp.maximum(i + 1, first * (2 - a) * BLK)
            allowed = (j >= low) & (j <= i + 2 * BLK)
            score = jnp.where(allowed, score, -jnp.inf)
            peak = jnp.max(score, axis=0, keepdims=True)
            terms = jnp.exp2((score - peak) * scale)
            sum_terms = jnp.sum(terms, axis=0, keepdims=True)
            got = dot(vals, terms.astype(BF16), ((1,), (0,)))
            got = (got * (1.0 / sum_terms)).astype(BF16)
            for h in range(4):
                head = got[:, h * BLK:(h + 1) * BLK]
                att[(4 * g + h) * HDIM:(4 * g + h + 1) * HDIM, a * BLK:(a + 1) * BLK] = head
                wide = head.astype(F32)
                sums[a] = sums[a] + jnp.sum(wide * wide, axis=0, keepdims=True)

        @pl.when(stays)
        def _():
            att_keep(g).start()

        @pl.when(jnp.logical_not(stays))
        def _():
            att_copy(g).start()

    sq_out[...] = jnp.broadcast_to(jnp.concatenate(sums, 1), (8, SPAN))

    def sq_copy(to, at):
        return pltpu.make_async_remote_copy(
            src_ref=sq_out, dst_ref=sq_in.at[at],
            send_sem=sq_send.at[to], recv_sem=sq_recv.at[at],
            device_id=(fz, fx, fy, fc, to), device_id_type=MESH,
        )

    def sq_keep():
        return pltpu.make_async_copy(sq_out, sq_in.at[hg], sq_recv.at[hg])

    for r in range(1, NH):
        sq_copy((hg + r) % NH, hg).start()

    @pl.when(stays)
    def _():
        sq_keep().start()

    @pl.when(jnp.logical_not(stays))
    def _():
        sq_copy(hg, hg).start()

    for r in range(1, NH):
        sq_copy((hg + r) % NH, (hg + r) % NH).wait_recv()

    @pl.when(stays)
    def _():
        sq_keep().wait()
        for g in range(2):
            att_keep(g).wait()

    @pl.when(jnp.logical_not(stays))
    def _():
        sq_copy(hg, hg).wait_recv()
        for g in range(2):
            att_copy(g).wait_recv()

    square = sq_in[0] + sq_in[1] + sq_in[2] + sq_in[3]
    rate = lax.rsqrt(square[0:1] / FEATS + 1e-06)

    def make_normed(k, carry):
        rows = pl.ds(pl.multiple_of(k * SDIM, SDIM), SDIM)
        gain = gcol[rows, :]
        value = att_in[rows, :].astype(F32) * jnp.concatenate([gain, gain], 1) * rate
        value = value.astype(BF16)
        normed[rows, :] = value
        weighted[rows, :] = (value.astype(F32) * w_v[k, 0:1, :]).astype(BF16)
        return carry

    lax.fori_loop(0, 16, make_normed, 0)
    states = dot(weighted[...], b_v[...], ((1,), (0,))).astype(BF16)
    for k in range(16):
        st_out[k] = states[k * SDIM:(k + 1) * SDIM]

    def st_copy(k, at):
        return pltpu.make_async_remote_copy(
            src_ref=st_out.at[k], dst_ref=st_in.at[at],
            send_sem=st_send.at[k], recv_sem=st_recv.at[at],
            device_id=plane_device(k), device_id_type=MESH,
        )

    def start_st(r, carry):
        st_copy((me + r) % PLANE, me).start()
        return carry

    lax.fori_loop(1, PLANE, start_st, 0)
    st_in[me] = st_out[me]

    def make_local(p, carry):
        lanes = pl.ds(pl.multiple_of(p * BLK, BLK), BLK)
        pair = []
        for h in range(2):
            k = 2 * p + h
            rows = pl.ds(pl.multiple_of(k * SDIM, SDIM), SDIM)
            value = normed[rows, :]
            pair.append(dot(value, mix[k], ((1,), (0,))) + value.astype(F32) * skip_ref[k])
        both = jnp.concatenate(pair, 0)
        for tb in range(2):
            part = slice(tb * BLK, (tb + 1) * BLK)
            local[part, lanes] = jnp.transpose(both[:, part])
        return carry

    lax.fori_loop(0, 8, make_local, 0)

    def wait_st(r, carry):
        st_copy((me + r) % PLANE, (me + r) % PLANE).wait_recv()
        return carry

    lax.fori_loop(1, PLANE, wait_st, 0)
    running = jnp.zeros((SDIM, STATE), F32)
    logs = jnp.zeros((8, 128), F32)
    for i in range(PLANE):
        pre_v[i] = running
        pre_log[i] = jnp.exp(logs)
        running = jnp.exp(tot_in[i][0:1]) * running + st_in[i].astype(F32)
        logs = logs + tot_in[i]
    run_out[...] = running.astype(BF16)
    run_in[z] = running.astype(BF16)

    def run_copy(to, at):
        return pltpu.make_async_remote_copy(
            src_ref=run_out, dst_ref=run_in.at[at],
            send_sem=run_send.at[to], recv_sem=run_recv.at[at],
            device_id=z_device(to), device_id_type=MESH,
        )

    def start_run(r, carry):
        run_copy((z + r) % NZ, z).start()
        return carry

    lax.fori_loop(1, NZ, start_run, 0)

    def wait_run(r, carry):
        run_copy((z + r) % NZ, (z + r) % NZ).wait_recv()
        log_copy((z + r) % NZ, (z + r) % NZ).wait_recv()
        return carry

    lax.fori_loop(1, NZ, wait_run, 0)
    carried = jnp.zeros((SDIM, STATE), F32)
    for i in range(NZ):
        later = jnp.exp(plane_in[i][0:1]) * carried + run_in[i].astype(F32)
        carried = jnp.where(i < z, later, carried)
    for i in range(PLANE):
        en_out[i] = (pre_v[i] + pre_log[i][0:1] * carried).astype(BF16)

    def en_copy(to, at):
        return pltpu.make_async_remote_copy(
            src_ref=en_out.at[to], dst_ref=en_in.at[at],
            send_sem=en_send.at[to], recv_sem=en_recv.at[at],
            device_id=plane_device(to), device_id_type=MESH,
        )

    def start_en(r, carry):
        en_copy((me + r) % PLANE, me).start()
        return carry

    lax.fori_loop(1, PLANE, start_en, 0)
    en_in[me] = en_out[me]

    def wait_en(r, carry):
        en_copy((me + r) % PLANE, (me + r) % PLANE).wait_recv()
        return carry

    lax.fori_loop(1, PLANE, wait_en, 0)
    entering = en_in[...].reshape(16 * SDIM, STATE)
    entry = dot(c_v[...], entering, ((1,), (1,)))
    out_ref[...] = (local[...] + ecum[...] * entry).astype(BF16)

    for g in range(2):
        for t in range(2):
            for slot in range(2):
                halo(t, g, slot).wait_send()
            swap(t, g).wait_send()
        q_swap(g).wait_send()
    for r in range(1, NH):
        sq_copy((hg + r) % NH, hg).wait_send()

    @pl.when(jnp.logical_not(stays))
    def _():
        sq_copy(hg, hg).wait_send()
        for g in range(2):
            att_copy(g).wait_send()

    def drain_plane(r, carry):
        to = (me + r) % PLANE
        tot_copy(to, me).wait_send()
        st_copy(to, me).wait_send()
        en_copy(to, me).wait_send()
        return carry

    lax.fori_loop(1, PLANE, drain_plane, 0)

    def drain_z(r, carry):
        to = (z + r) % NZ
        log_copy(to, z).wait_send()
        run_copy(to, z).wait_send()
        return carry

    lax.fori_loop(1, NZ, drain_z, 0)


def body(query, keys, values, norm_gain, in_b, out_c, step, log_decay, skip):
    feats = query.shape[2]
    gain = norm_gain.reshape(feats // HDIM, HDIM)
    dma = pltpu.SemaphoreType.DMA
    vm = pltpu.VMEM
    scratch = [
        vm((2, BLK, feats), BF16),
        vm((2, BLK, 256), BF16),
        vm((2, BLK, 256), BF16),
        vm((4 * BLK, 256), BF16),
        vm((4 * BLK, 256), BF16),
        vm((8, HDIM), F32),
        vm((SPAN, STATE), BF16),
        vm((SPAN, STATE), BF16),
        vm((16, SPAN), F32),
        vm((16, SPAN), F32),
        vm((16, 8, SPAN), F32),
        vm((16, 8, SPAN), F32),
        vm((16, 8, SPAN), F32),
        vm((feats, 128), F32),
        vm((16, SPAN, SPAN), BF16),
        vm((SPAN, feats), F32),
        vm((feats, SPAN), BF16),
        vm((feats, SPAN), BF16),
        vm((8, SPAN), F32),
        vm((NH, 8, SPAN), F32),
        vm((feats, SPAN), BF16),
        vm((feats, SPAN), BF16),
        vm((SPAN, feats), F32),
        vm((16, 8, 128), F32),
        vm((PLANE, 8, 128), F32),
        vm((8, 128), F32),
        vm((NZ, 8, 128), F32),
        vm((16, SDIM, STATE), BF16),
        vm((PLANE, SDIM, STATE), BF16),
        vm((PLANE, SDIM, STATE), F32),
        vm((PLANE, 8, 128), F32),
        vm((SDIM, STATE), BF16),
        vm((NZ, SDIM, STATE), BF16),
        vm((PLANE, SDIM, STATE), BF16),
        vm((16, SDIM, STATE), BF16),
        dma((10,)),
        dma((2, 2, 2)), dma((2, 2, 2)),
        dma((2, 2)), dma((2, 2)),
        dma((2,)), dma((2,)),
        dma((2,)), dma((2,)),
        dma((NH,)), dma((NH,)),
        dma((PLANE,)), dma((PLANE,)),
        dma((NZ,)), dma((NZ,)),
        dma((PLANE,)), dma((PLANE,)),
        dma((NZ,)), dma((NZ,)),
        dma((NZ,)), dma((NZ,)),
        dma((PLANE,)), dma((PLANE,)),
    ]
    anywhere = pl.BlockSpec(memory_space=pl.ANY)
    return pl.pallas_call(
        kernel,
        out_shape=jax.ShapeDtypeStruct((SPAN, feats), BF16),
        in_specs=[anywhere] * 8 + [pl.BlockSpec(memory_space=pltpu.SMEM)],
        out_specs=pl.BlockSpec(memory_space=pltpu.VMEM),
        scratch_shapes=scratch,
        compiler_params=pltpu.CompilerParams(collective_id=0, has_side_effects=True),
    )(query, keys, values, gain, in_b, out_c, step, log_decay, skip)


def solution(mesh):
    torus = Mesh(mesh.devices.reshape(NZ, NX, NY, NC, NH), AXES)
    return jax.shard_map(
        body,
        mesh=torus,
        in_specs=(
            P(None, SEQ, "head"),
            P(None, SEQ, "head"),
            P(None, SEQ, "head"),
            P("head"),
            P(SEQ, None),
            P(SEQ, None),
            P("head", SEQ),
            P("head", SEQ),
            P("head"),
        ),
        out_specs=P(SEQ, "head"),
        check_vma=False,
    )
```

time: 224 us -> 99.7 us (0.45); the launches traced: 220 us -> 99.5 us
  Pallas kernels: 0 us -> 97.6 us
  waiting for transfers between devices: 87 us -> 0 us
  starting transfers between devices: 56.7 us -> 0 us
  blocking collectives: 42.1 us -> 0 us
  between operations: 14.1 us -> 0.01 us
  matrix products: 7.69 us -> 0 us
  other arithmetic: 5.95 us -> 0 us
  local copies, waits for them, and re-layouts: 6.52 us -> 1.87 us
    pallas_call x0 -> x1, Pallas kernels: none -> 97.6 us  [body(): pl.pallas_call(kernel, out_shape=jax.ShapeDtypeStruct((SPAN, feats), BF16...]
    ppermute x11 -> x0, starting transfers between devices: 50.9 us -> none  [the longest x7 37.6 us: partner(): return lax.ppermute(block, axis, route)]
    all_gather x2 -> x0, waiting for transfers between devices: 45.4 us -> none  [prefix_by_axis(): lax.all_gather(part.astype(kind), axis)]
    all_gather x6 -> x0, blocking collectives: 42.1 us -> none  [prefix_by_axis(): lax.all_gather(part.astype(kind), axis)]
    ppermute x11 -> x0, waiting for transfers between devices: 35.1 us -> none  [the longest x7 29.3 us: partner(): return lax.ppermute(block, axis, route)]
    dot_general x8 -> x0, matrix products: 7.69 us -> none  [the longest x1 3.59 us: body(): jnp.einsum('ctn,chen->cthe', out_rows, starts, precision=highest)]
    all_to_all x1 -> x0, waiting for transfers between devices: 6.46 us -> none  [copy_for_each(): return lax.all_to_all(copies, axis, split_axis=0, concat_axis=0, tiled=True)]
    all_to_all x1 -> x0, starting transfers between devices: 5.76 us -> none  [copy_for_each(): return lax.all_to_all(copies, axis, split_axis=0, concat_axis=0, tiled=True)]
  transfers between devices with their start and end apart: 14 -> 0, of which waited for: 11 -> 0; matrix products, arithmetic and copies ran while one was open for 2% -> 0% of each run, Pallas kernels for 0% -> 0%
where the time goes in v1:
time: 99.7 us; the launch traced here: 99.5 us
  Pallas kernels  97.6 us (98%)
  local copies, waits for them, and re-layouts  1.87 us (2%)
    pallas_call x1, Pallas kernels, body(): pl.pallas_call(kernel, out_shape=jax.ShapeDtypeStruct((SPAN, feats), BF16...  97.6 us

profile of v1, /device:TPU:1, one launch (start us, length us, event | category | flops | bytes accessed | tf_op | source)
XLA Modules:
  0.0 99.5 jit_solution(5695890534086815691)
XLA Ops:
  0.0 97.6 %shard_map.91 = bf16[256,1024]{1,0:T(8,128)(2,1)} custom-call(bf16[2,128,1024]{2,1,0:T(8,128)(2,1)} %q_hbm.1, bf16[2,128,256]{2,1,0:T(8,128)(2,1)} %k_hbm.1, bf16[2,128,256]{2,1,0:T(8,128)(2,1)} %v_hbm.1, f32[8,128]{1,0:T(8,128)} %bitcast.1, bf16[256,128]{1,0:T(8,128)(2,1)} %b_hbm.1, bf16[256,128]{1,0:T(8,128)(2,1)} %c_hbm.1, f32[16,256]{1,0:T(8,128)} %step_hbm.1, ...), custom_call_target="tpu_custom_call" | custom-call | tf_op jit(solution)/shard_map/pallas_call | solution.py:554
  97.6 1.9 %copy.11 = bf16[256,1024]{1,0:T(8,128)(2,1)} copy(bf16[256,1024]{1,0:T(8,128)(2,1)} %shard_map.91) | data formatting | bytes 1048576

commit v2 on v1

v2 whole, which is shorter than its diff:
```python
import math

import jax
import jax.numpy as jnp
from jax import lax
from jax.experimental import pallas as pl
from jax.experimental.pallas import tpu as pltpu
from jax.sharding import Mesh
from jax.sharding import PartitionSpec as P

HDIM = 128
SDIM = 64
STATE = 128
SPAN = 256
BLK = 128
FEATS = 4096
NZ, NX, NY, NC, NH = 8, 4, 2, 2, 4
CHIPS = NZ * NX * NY
PLANE = NX * NY * NC
CHUNKS = 4
WIDE = 256
SLICE = 16
AXES = ("z", "x", "y", "core", "head")
SEQ = ("z", "x", "y", "core")
MESH = pl.DeviceIdType.MESH
F32 = jnp.float32
BF16 = jnp.bfloat16


def chip_coords(chip):
    return chip // (NX * NY), (chip // NY) % NX, chip % NY


def seq_coords(index):
    return index // PLANE, (index // (NY * NC)) % NX, (index // NC) % NY, index % NC


def dot(a, b, dims, **kw):
    return lax.dot_general(a, b, (dims, ((), ())), preferred_element_type=F32, **kw)


def kernel(
    q_hbm, k_hbm, v_hbm, gain_hbm, b_hbm, c_hbm, step_hbm, decay_hbm, skip_ref,
    out_ref,
    q_span, k_stage, v_stage, k_win, v_win, gain_v, b_v, c_v, step_v, decay_v,
    cum_v, w_v, v_v, gcol, mix, ecum, att, z_in, att_in, sq_out, sq_in, normed, weighted, local,
    tot_out, tot_in, decays, starts, plane_out, plane_in, plane_decay,
    st_out, st_in, pre_v, run_out, run_in, en_out, en_in,
    load_sem, halo_send, halo_recv, swap_send, swap_recv, q_send, q_recv, z_send, z_recv,
    att_send, att_recv, sq_send, sq_recv, tot_send, tot_recv, log_send, log_recv,
    st_send, st_recv, run_send, run_recv, en_send, en_recv,
):
    z, x, y, core, hg = (lax.axis_index(a) for a in AXES)
    chip = (z * NX + x) * NY + y
    me = (x * NY + y) * NC + core
    other = 1 - core
    partner = (z, x, y, other, hg)

    after = (chip + 1) % CHIPS
    az, ax, ay = chip_coords(after)
    wraps = (chip == CHIPS - 1).astype(jnp.int32)
    before = (chip + CHIPS - 1) % CHIPS
    bz, bx, by = chip_coords(before)

    span = core * CHIPS + chip
    fz, fx, fy, fc = seq_coords(span)
    seq = z * PLANE + me
    sz, sx, sy = chip_coords(seq % CHIPS)
    sc = seq // CHIPS
    stays = span == seq
    z_to = (NZ // 2 * core + z // 2, x, y, z % 2, hg)
    z_from = (2 * (z % (NZ // 2)) + core, x, y, z // (NZ // 2), hg)
    z_stays = jnp.logical_and(z_to[0] == z, z_to[3] == core)
    p_to = (z, 2 * core + x // 2, x % 2, y, hg)
    p_from = (z, 2 * (x % 2) + y, core, x // 2, hg)
    p_stays = jnp.logical_and(p_to[1] == x, jnp.logical_and(p_to[2] == y, p_to[3] == core))

    mine = pl.ds(pl.multiple_of((2 + core) * BLK, BLK), BLK)
    theirs = pl.ds(pl.multiple_of((2 + other) * BLK, BLK), BLK)
    prev_row = pl.ds(pl.multiple_of(core * BLK, BLK), BLK)
    loads = [
        (decay_hbm, decay_v), (step_hbm, step_v), (k_hbm, k_stage), (v_hbm, v_stage),
        (k_hbm.at[core], k_win.at[mine]), (v_hbm.at[core], v_win.at[mine]),
        (q_hbm.at[core], q_span.at[core]),
        (b_hbm, b_v), (c_hbm, c_v), (gain_hbm, gain_v),
    ]
    loads = [pltpu.make_async_copy(s, d, load_sem.at[i]) for i, (s, d) in enumerate(loads)]
    for copy in loads:
        copy.start()

    barrier = pltpu.get_barrier_semaphore()

    def greet(device):
        pl.semaphore_signal(barrier, inc=1, device_id=device, device_id_type=MESH)

    def plane_device(index):
        return (z, index // (NY * NC), (index // NC) % NY, index % NC, hg)

    def z_device(index):
        return (index, x, y, core, hg)

    for c in range(NC):
        greet((bz, bx, by, c, hg))

    def greet_plane(r, carry):
        greet(plane_device((me + r) % PLANE))
        return carry

    lax.fori_loop(1, PLANE, greet_plane, 0)

    def greet_z(r, carry):
        greet(z_device((z + r) % NZ))
        return carry

    lax.fori_loop(1, NZ, greet_z, 0)

    @pl.when(jnp.logical_not(z_stays))
    def _():
        greet(z_from)

    for r in range(1, NH):
        greet((sz, sx, sy, sc, (hg + r) % NH))

    @pl.when(jnp.logical_not(stays))
    def _():
        greet((sz, sx, sy, sc, hg))

    loads[0].wait()
    loads[1].wait()
    row = lax.broadcasted_iota(jnp.int32, (SPAN, SPAN), 0)
    col = lax.broadcasted_iota(jnp.int32, (SPAN, SPAN), 1)
    causal = row <= col
    cum = dot(decay_v[...], causal.astype(F32), ((1,), (0,)), precision=lax.Precision.HIGHEST)
    total = cum[:, SPAN - 1:]
    tail = jnp.exp(total - cum) * step_v[...]
    shift = jnp.log(step_v[...]) - cum
    for k in range(16):
        cum_v[k] = jnp.broadcast_to(cum[k:k + 1], (8, SPAN))
        w_v[k] = jnp.broadcast_to(tail[k:k + 1], (8, SPAN))
        v_v[k] = jnp.broadcast_to(shift[k:k + 1], (8, SPAN))
    for o in range(4):
        lines = [total[4 * (n % 4) + o:4 * (n % 4) + o + 1] for n in range(8)]
        tot_out[o] = jnp.broadcast_to(jnp.concatenate(lines, 0), (8, 128))
    for copy in loads[2:]:
        copy.wait()

    moves = jnp.logical_not(stays).astype(jnp.int32) + jnp.logical_not(z_stays).astype(jnp.int32)
    pl.semaphore_wait(barrier, NC + NH - 1 + PLANE - 1 + NZ - 1 + moves)

    def remote(src, dst, send, recv, to):
        return pltpu.make_async_remote_copy(
            src_ref=src, dst_ref=dst, send_sem=send, recv_sem=recv,
            device_id=to, device_id_type=MESH,
        )

    def cols(g, width=HDIM):
        return pl.ds(g * width, width)

    def halo(i, g, slot):
        stage, window = ((k_stage, k_win), (v_stage, v_win))[i]
        to = (az, ax, ay, jnp.where(wraps == 1, 1 - slot, slot), hg)
        return remote(
            stage.at[slot, :, cols(g)], window.at[prev_row, cols(g)],
            halo_send.at[i, g, slot], halo_recv.at[i, g, core], to,
        )

    def halo_arrival(i, g, block):
        part = (k_win, v_win)[i].at[pl.ds(block * BLK, BLK), cols(g)]
        return remote(part, part, halo_send.at[i, g, 0], halo_recv.at[i, g, block], partner)

    def swap(i, g):
        stage, window = ((k_stage, k_win), (v_stage, v_win))[i]
        return remote(
            stage.at[other, :, cols(g)], window.at[mine, cols(g)],
            swap_send.at[i, g], swap_recv.at[i, g], partner,
        )

    def swap_arrival(i, g):
        part = (k_win, v_win)[i].at[theirs, cols(g)]
        return remote(part, part, swap_send.at[i, g], swap_recv.at[i, g], partner)

    def q_swap(g):
        return remote(
            q_hbm.at[other, :, cols(g, 512)], q_span.at[core, :, cols(g, 512)],
            q_send.at[g], q_recv.at[g], partner,
        )

    def q_arrival(g):
        part = q_span.at[other, :, cols(g, 512)]
        return remote(part, part, q_send.at[g], q_recv.at[g], partner)

    for g in range(2):
        for i in range(2):
            for slot in range(2):
                halo(i, g, slot).start()
        q_swap(g).start()
        for i in range(2):
            swap(i, g).start()

    def tot_copy(to, at):
        return remote(
            tot_out.at[to // 4], tot_in.at[at], tot_send.at[to], tot_recv.at[at], plane_device(to)
        )

    def start_tot(r, carry):
        tot_copy((me + r) % PLANE, me).start()
        return carry

    lax.fori_loop(1, PLANE, start_tot, 0)
    tot_in[me] = tot_out[me // 4]
    for p in range(8):
        line = jnp.broadcast_to(gain_v[p:p + 1, :], (BLK, BLK))
        gcol[p * BLK:(p + 1) * BLK, :] = jnp.transpose(line)

    scale = math.log2(math.e) / math.sqrt(HDIM)
    j = lax.broadcasted_iota(jnp.int32, (3 * BLK, 2 * BLK), 0)
    i = lax.broadcasted_iota(jnp.int32, (3 * BLK, 2 * BLK), 1) % BLK
    first = (span == 0).astype(jnp.int32)

    def part(q):
        return pl.ds(q * WIDE, WIDE)

    def z_copy(q):
        return remote(att.at[part(q)], z_in.at[part(q)], z_send.at[q], z_recv.at[q], z_to)

    def z_keep(q):
        return pltpu.make_async_copy(att.at[part(q)], z_in.at[part(q)], z_recv.at[q])

    def p_copy(q):
        return remote(z_in.at[part(q)], att_in.at[part(q)], att_send.at[q], att_recv.at[q], p_to)

    def p_keep(q):
        return pltpu.make_async_copy(z_in.at[part(q)], att_in.at[part(q)], att_recv.at[q])

    def either(here, keep, leave):
        @pl.when(here)
        def _():
            keep()

        @pl.when(jnp.logical_not(here))
        def _():
            leave()

    def sq_copy(to, at):
        return remote(
            sq_out, sq_in.at[at], sq_send.at[to], sq_recv.at[at], (fz, fx, fy, fc, to)
        )

    def sq_keep():
        return pltpu.make_async_copy(sq_out, sq_in.at[hg], sq_recv.at[hg])

    sums = [jnp.zeros((1, BLK), F32) for _ in range(2)]
    for q in range(CHUNKS):
        g = q // 2
        if q % 2 == 0:
            for t in range(2):
                for block in range(2):
                    halo_arrival(t, g, block).wait_recv()
                swap_arrival(t, g).wait_recv()
            q_arrival(g).wait_recv()
        lanes = slice(g * HDIM, (g + 1) * HDIM)
        for a in range(2):
            keys = k_win[a * BLK:(a + 3) * BLK, lanes]
            vals = jnp.transpose(v_win[a * BLK:(a + 3) * BLK, lanes])
            heads = [q_span[a, :, (2 * q + h) * HDIM:(2 * q + h + 1) * HDIM] for h in range(2)]
            score = dot(keys, jnp.concatenate(heads, 0), ((1,), (1,)))
            low = jnp.maximum(i + 1, first * (2 - a) * BLK)
            allowed = (j >= low) & (j <= i + 2 * BLK)
            score = jnp.where(allowed, score, -jnp.inf)
            peak = jnp.max(score, axis=0, keepdims=True)
            terms = jnp.exp2((score - peak) * scale)
            sum_terms = jnp.sum(terms, axis=0, keepdims=True)
            got = dot(vals, terms.astype(BF16), ((1,), (0,)))
            got = (got * (1.0 / sum_terms)).astype(BF16)
            for h in range(2):
                head = got[:, h * BLK:(h + 1) * BLK]
                att[(2 * q + h) * HDIM:(2 * q + h + 1) * HDIM, a * BLK:(a + 1) * BLK] = head
                wide = head.astype(F32)
                sums[a] = sums[a] + jnp.sum(wide * wide, axis=0, keepdims=True)
        if q == 0:
            either(z_stays, z_keep(0).start, z_copy(0).start)

    sq_out[...] = jnp.broadcast_to(jnp.concatenate(sums, 1), (8, SPAN))
    for r in range(1, NH):
        sq_copy((hg + r) % NH, hg).start()
    either(stays, sq_keep().start, sq_copy(hg, hg).start)
    for q in range(1, CHUNKS):
        either(z_stays, z_keep(q).start, z_copy(q).start)

    cross = dot(b_v[...], c_v[...], ((1,), (1,)))

    def make_mix(k, carry):
        ct = cum_v[k, 0:1, :]
        for ub in range(2):
            line = v_v[k, 0:1, ub * BLK:(ub + 1) * BLK]
            colb = jnp.transpose(jnp.broadcast_to(line, (BLK, BLK)))
            arg = ct + jnp.concatenate([colb, colb], 1)
            rows = slice(ub * BLK, (ub + 1) * BLK)
            arg = jnp.where(causal[rows], arg, -jnp.inf)
            mix[k, rows] = (jnp.exp(arg) * cross[rows]).astype(BF16)
        return carry

    lax.fori_loop(0, 16, make_mix, 0)

    def make_ecum(p, carry):
        lanes = pl.ds(pl.multiple_of(p * BLK, BLK), BLK)
        for tb in range(2):
            half = slice(tb * BLK, (tb + 1) * BLK)
            pair = [
                jnp.broadcast_to(jnp.exp(cum_v[2 * p + h, 0:1, half]), (SDIM, BLK))
                for h in range(2)
            ]
            ecum[half, lanes] = jnp.transpose(jnp.concatenate(pair, 0))
        return carry

    lax.fori_loop(0, 8, make_ecum, 0)

    def wait_tot(r, carry):
        tot_copy((me + r) % PLANE, (me + r) % PLANE).wait_recv()
        return carry

    lax.fori_loop(1, PLANE, wait_tot, 0)
    logs = jnp.zeros((8, 128), F32)
    for n in range(PLANE):
        starts[n] = jnp.exp(logs)
        decays[n] = jnp.exp(tot_in[n])
        logs = logs + tot_in[n]
    plane_out[...] = logs
    plane_in[z] = logs

    def log_copy(to, at):
        return remote(plane_out, plane_in.at[at], log_send.at[to], log_recv.at[at], z_device(to))

    def start_log(r, carry):
        log_copy((z + r) % NZ, z).start()
        return carry

    lax.fori_loop(1, NZ, start_log, 0)

    def st_copy(q, to, at):
        return remote(
            st_out.at[q, to], st_in.at[q, at], st_send.at[q, to], st_recv.at[q, at],
            plane_device(to),
        )

    def run_copy(q, to, at):
        return remote(
            run_out.at[q], run_in.at[q, at], run_send.at[q, to], run_recv.at[q, at], z_device(to)
        )

    def en_copy(q, to, at):
        return remote(
            en_out.at[q, to], en_in.at[q, at], en_send.at[q, to], en_recv.at[q, at],
            plane_device(to),
        )

    def ring(count, own, act):
        def visit(r, carry):
            act((own + r) % count)
            return carry

        lax.fori_loop(1, count, visit, 0)

    def arrive(q):
        either(z_stays, z_keep(q).wait, z_copy(q).wait_recv)
        either(p_stays, p_keep(q).start, p_copy(q).start)

    def states(q):
        if q == 0:
            for r in range(1, NH):
                sq_copy((hg + r) % NH, (hg + r) % NH).wait_recv()
            either(stays, sq_keep().wait, sq_copy(hg, hg).wait_recv)
        either(p_stays, p_keep(q).wait, p_copy(q).wait_recv)
        square = sq_in[0] + sq_in[1] + sq_in[2] + sq_in[3]
        rate = lax.rsqrt(square[0:1] / FEATS + 1e-06)

        def make_normed(k, carry):
            rows = pl.ds(pl.multiple_of(k * SDIM, SDIM), SDIM)
            gain = gcol[rows, :]
            value = att_in[rows, :].astype(F32) * jnp.concatenate([gain, gain], 1) * rate
            value = value.astype(BF16)
            normed[rows, :] = value
            weighted[rows, :] = (value.astype(F32) * w_v[k, 0:1, :]).astype(BF16)
            return carry

        lax.fori_loop(4 * q, 4 * q + 4, make_normed, 0)
        state = dot(weighted[q * WIDE:(q + 1) * WIDE], b_v[...], ((1,), (0,)))
        st_out[q] = state.astype(BF16).reshape(PLANE, SLICE, STATE)
        ring(PLANE, me, lambda to: st_copy(q, to, me).start())
        st_in[q, me] = st_out[q, me]

        def make_local(p, carry):
            lanes = pl.ds(pl.multiple_of(p * BLK, BLK), BLK)
            pair = []
            for h in range(2):
                k = 2 * p + h
                rows = pl.ds(pl.multiple_of(k * SDIM, SDIM), SDIM)
                value = normed[rows, :]
                pair.append(dot(value, mix[k], ((1,), (0,))) + value.astype(F32) * skip_ref[k])
            both = jnp.concatenate(pair, 0)
            for tb in range(2):
                half = slice(tb * BLK, (tb + 1) * BLK)
                local[half, lanes] = jnp.transpose(both[:, half])
            return carry

        lax.fori_loop(2 * q, 2 * q + 2, make_local, 0)

    def prefix(q):
        ring(PLANE, me, lambda at: st_copy(q, at, at).wait_recv())
        running = jnp.zeros((SLICE, STATE), F32)
        for n in range(PLANE):
            pre_v[q, n] = running
            running = decays[n, q:q + 1] * running + st_in[q, n].astype(F32)
        run_out[q] = running.astype(BF16)
        ring(NZ, z, lambda to: run_copy(q, to, z).start())
        run_in[q, z] = running.astype(BF16)

    def enter(q):
        if q == 0:
            ring(NZ, z, lambda at: log_copy(at, at).wait_recv())
            for n in range(NZ):
                plane_decay[n] = jnp.exp(plane_in[n])
        ring(NZ, z, lambda at: run_copy(q, at, at).wait_recv())
        carried = jnp.zeros((SLICE, STATE), F32)
        for n in range(NZ):
            later = plane_decay[n, q:q + 1] * carried + run_in[q, n].astype(F32)
            carried = jnp.where(n < z, later, carried)
        for n in range(PLANE):
            en_out[q, n] = (pre_v[q, n] + starts[n, q:q + 1] * carried).astype(BF16)
        ring(PLANE, me, lambda to: en_copy(q, to, me).start())
        en_in[q, me] = en_out[q, me]

    def finish(q):
        ring(PLANE, me, lambda at: en_copy(q, at, at).wait_recv())
        lanes = slice(q * WIDE, (q + 1) * WIDE)
        entry = dot(c_v[...], en_in[q].reshape(WIDE, STATE), ((1,), (1,)))
        out_ref[:, lanes] = (local[:, lanes] + ecum[:, lanes] * entry).astype(BF16)

    for t in range(CHUNKS + 4):
        for lag, stage in ((4, finish), (3, enter), (2, prefix), (1, states), (0, arrive)):
            if 0 <= t - lag < CHUNKS:
                stage(t - lag)

    for g in range(2):
        for t in range(2):
            for slot in range(2):
                halo(t, g, slot).wait_send()
            swap(t, g).wait_send()
        q_swap(g).wait_send()
    for r in range(1, NH):
        sq_copy((hg + r) % NH, hg).wait_send()

    @pl.when(jnp.logical_not(stays))
    def _():
        sq_copy(hg, hg).wait_send()

    @pl.when(jnp.logical_not(z_stays))
    def _():
        for q in range(CHUNKS):
            z_copy(q).wait_send()

    @pl.when(jnp.logical_not(p_stays))
    def _():
        for q in range(CHUNKS):
            p_copy(q).wait_send()

    ring(PLANE, me, lambda to: tot_copy(to, me).wait_send())
    ring(NZ, z, lambda to: log_copy(to, z).wait_send())
    for q in range(CHUNKS):
        ring(PLANE, me, lambda to: st_copy(q, to, me).wait_send())
        ring(NZ, z, lambda to: run_copy(q, to, z).wait_send())
        ring(PLANE, me, lambda to: en_copy(q, to, me).wait_send())


def body(query, keys, values, norm_gain, in_b, out_c, step, log_decay, skip):
    feats = query.shape[2]
    gain = norm_gain.reshape(feats // HDIM, HDIM)
    dma = pltpu.SemaphoreType.DMA
    vm = pltpu.VMEM
    scratch = [
        vm((2, BLK, feats), BF16),
        vm((2, BLK, 256), BF16),
        vm((2, BLK, 256), BF16),
        vm((4 * BLK, 256), BF16),
        vm((4 * BLK, 256), BF16),
        vm((8, HDIM), F32),
        vm((SPAN, STATE), BF16),
        vm((SPAN, STATE), BF16),
        vm((16, SPAN), F32),
        vm((16, SPAN), F32),
        vm((16, 8, SPAN), F32),
        vm((16, 8, SPAN), F32),
        vm((16, 8, SPAN), F32),
        vm((feats, 128), F32),
        vm((16, SPAN, SPAN), BF16),
        vm((SPAN, feats), F32),
        vm((feats, SPAN), BF16),
        vm((feats, SPAN), BF16),
        vm((feats, SPAN), BF16),
        vm((8, SPAN), F32),
        vm((NH, 8, SPAN), F32),
        vm((feats, SPAN), BF16),
        vm((feats, SPAN), BF16),
        vm((SPAN, feats), F32),
        vm((4, 8, 128), F32),
        vm((PLANE, 8, 128), F32),
        vm((PLANE, 8, 128), F32),
        vm((PLANE, 8, 128), F32),
        vm((8, 128), F32),
        vm((NZ, 8, 128), F32),
        vm((NZ, 8, 128), F32),
        vm((CHUNKS, PLANE, SLICE, STATE), BF16),
        vm((CHUNKS, PLANE, SLICE, STATE), BF16),
        vm((CHUNKS, PLANE, SLICE, STATE), F32),
        vm((CHUNKS, SLICE, STATE), BF16),
        vm((CHUNKS, NZ, SLICE, STATE), BF16),
        vm((CHUNKS, PLANE, SLICE, STATE), BF16),
        vm((CHUNKS, PLANE, SLICE, STATE), BF16),
        dma((10,)),
        dma((2, 2, 2)), dma((2, 2, 2)),
        dma((2, 2)), dma((2, 2)),
        dma((2,)), dma((2,)),
        dma((CHUNKS,)), dma((CHUNKS,)),
        dma((CHUNKS,)), dma((CHUNKS,)),
        dma((NH,)), dma((NH,)),
        dma((PLANE,)), dma((PLANE,)),
        dma((NZ,)), dma((NZ,)),
        dma((CHUNKS, PLANE)), dma((CHUNKS, PLANE)),
        dma((CHUNKS, NZ)), dma((CHUNKS, NZ)),
        dma((CHUNKS, PLANE)), dma((CHUNKS, PLANE)),
    ]
    anywhere = pl.BlockSpec(memory_space=pl.ANY)
    return pl.pallas_call(
        kernel,
        out_shape=jax.ShapeDtypeStruct((SPAN, feats), BF16),
        in_specs=[anywhere] * 8 + [pl.BlockSpec(memory_space=pltpu.SMEM)],
        out_specs=pl.BlockSpec(memory_space=pltpu.VMEM),
        scratch_shapes=scratch,
        compiler_params=pltpu.CompilerParams(collective_id=0, has_side_effects=True),
    )(query, keys, values, gain, in_b, out_c, step, log_decay, skip)


def solution(mesh):
    torus = Mesh(mesh.devices.reshape(NZ, NX, NY, NC, NH), AXES)
    return jax.shard_map(
        body,
        mesh=torus,
        in_specs=(
            P(None, SEQ, "head"),
            P(None, SEQ, "head"),
            P(None, SEQ, "head"),
            P("head"),
            P(SEQ, None),
            P(SEQ, None),
            P("head", SEQ),
            P("head", SEQ),
            P("head"),
        ),
        out_specs=P(SEQ, "head"),
        check_vma=False,
    )
```

time: 99.7 us -> 93 us (0.933)
  Pallas kernels: 97.6 us -> 91 us
    pallas_call x1, Pallas kernels: 97.6 us -> 91 us  [body(): pl.pallas_call(kernel, out_shape=jax.ShapeDtypeStruct((SPAN, feats), BF16...]
where the time goes in v2:
time: 93 us; the launch traced here: 92.9 us
  Pallas kernels  91 us (98%)
  local copies, waits for them, and re-layouts  1.87 us (2%)
    pallas_call x1, Pallas kernels, body(): pl.pallas_call(kernel, out_shape=jax.ShapeDtypeStruct((SPAN, feats), BF16...  91 us
    unnamed x1, local copies, waits for them, and re-layouts  1.87 us

profile of v2, /device:TPU:1, one launch (start us, length us, event | category | flops | bytes accessed | tf_op | source)
XLA Modules:
  0.0 92.9 jit_solution(2222351876261788669)
XLA Ops:
  0.0 91.0 %shard_map.91 = bf16[256,1024]{1,0:T(8,128)(2,1)} custom-call(bf16[2,128,1024]{2,1,0:T(8,128)(2,1)} %q_hbm.1, bf16[2,128,256]{2,1,0:T(8,128)(2,1)} %k_hbm.1, bf16[2,128,256]{2,1,0:T(8,128)(2,1)} %v_hbm.1, f32[8,128]{1,0:T(8,128)} %bitcast.1, bf16[256,128]{1,0:T(8,128)(2,1)} %b_hbm.1, bf16[256,128]{1,0:T(8,128)(2,1)} %c_hbm.1, f32[16,256]{1,0:T(8,128)} %step_hbm.1, ...), custom_call_target="tpu_custom_call" | custom-call | tf_op jit(solution)/shard_map/pallas_call | solution.py:533
  91.0 1.9 %copy.11 = bf16[256,1024]{1,0:T(8,128)(2,1)} copy(bf16[256,1024]{1,0:T(8,128)(2,1)} %shard_map.91) | data formatting | bytes 1048576

commit v3 on v2

v3 whole, which is shorter than its diff:
```python
import math

import jax
import jax.numpy as jnp
from jax import lax
from jax.experimental import pallas as pl
from jax.experimental.pallas import tpu as pltpu
from jax.sharding import Mesh
from jax.sharding import PartitionSpec as P

HDIM = 128
SDIM = 64
STATE = 128
SPAN = 256
BLK = 128
FEATS = 4096
NZ, NX, NY, NC, NH = 8, 4, 2, 2, 4
CHIPS = NZ * NX * NY
PLANE = NX * NY * NC
CHUNKS = 4
WIDE = 256
HALVES = 2
HALF = 512
SLICE = 32
AXES = ("z", "x", "y", "core", "head")
SEQ = ("z", "x", "y", "core")
MESH = pl.DeviceIdType.MESH
F32 = jnp.float32
BF16 = jnp.bfloat16


def chip_coords(chip):
    return chip // (NX * NY), (chip // NY) % NX, chip % NY


def seq_coords(index):
    return index // PLANE, (index // (NY * NC)) % NX, (index // NC) % NY, index % NC


def dot(a, b, dims, **kw):
    return lax.dot_general(a, b, (dims, ((), ())), preferred_element_type=F32, **kw)


def kernel(
    q_hbm, k_hbm, v_hbm, gain_hbm, b_hbm, c_hbm, step_hbm, decay_hbm, skip_ref,
    out_ref,
    q_span, k_stage, v_stage, k_win, v_win, gain_v, b_v, c_v, step_v, decay_v,
    cum_v, w_v, v_v, gcol, mix, ecum, att, z_in, att_in, sq_out, sq_mid, sq_in, normed, weighted, local,
    tot_out, tot_in, decays, starts, plane_out, plane_in,
    st_out, st_in, pre_v, run_out, run_in, en_out, en_in,
    load_sem, halo_send, halo_recv, swap_send, swap_recv, q_send, q_recv, z_send, z_recv,
    relay_send, att_send, att_recv, sqz_send, sqz_recv, sqr_send, sq_send, sq_recv,
    tot_send, tot_recv, log_send, log_recv, st_send, st_recv, run_send, run_recv,
    en_send, en_recv, ready_sem, later_sem,
):
    z, x, y, core, hg = (lax.axis_index(a) for a in AXES)
    chip = (z * NX + x) * NY + y
    me = (x * NY + y) * NC + core
    other = 1 - core
    partner = (z, x, y, other, hg)

    after = (chip + 1) % CHIPS
    az, ax, ay = chip_coords(after)
    wraps = (chip == CHIPS - 1).astype(jnp.int32)
    before = (chip + CHIPS - 1) % CHIPS
    bz, bx, by = chip_coords(before)

    span = core * CHIPS + chip
    long_out = z == jnp.where(core == 0, NZ - 1, 0)
    long_out = jnp.where(long_out, 1, 0)
    relays = jnp.where(z == jnp.where(core == 0, 1, NZ - 2), 1, 0)
    long_in = jnp.where(z == jnp.where(core == 0, NZ // 2, NZ // 2 - 1), 1, 0)
    relay_of = jnp.where(core == 0, 1, NZ - 2)
    to_z = jnp.where(long_out == 1, relay_of, NZ // 2 * core + z // 2)
    to_core = jnp.where(long_out == 1, core, z % 2)
    z_to = (to_z, x, y, to_core, hg)
    from_z = jnp.where(long_in == 1, jnp.where(core == 0, NZ - 2, 1), 2 * (z % (NZ // 2)) + core)
    from_core = jnp.where(long_in == 1, other, z // (NZ // 2))
    z_from = (from_z, x, y, from_core, hg)
    relay_from = (jnp.where(core == 0, NZ - 1, 0), x, y, core, hg)
    relay_to = (jnp.where(core == 0, NZ // 2 - 1, NZ // 2), x, y, other, hg)
    z_stays = jnp.logical_and(to_z == z, to_core == core)
    z_moves = jnp.logical_not(z_stays)
    relaying = relays == 1
    p_to = (z, 2 * core + x // 2, x % 2, y, hg)
    p_from = (z, 2 * (x % 2) + y, core, x // 2, hg)
    p_stays = jnp.logical_and(p_to[1] == x, jnp.logical_and(p_to[2] == y, p_to[3] == core))
    p_moves = jnp.logical_not(p_stays)

    mine = pl.ds(pl.multiple_of((2 + core) * BLK, BLK), BLK)
    theirs = pl.ds(pl.multiple_of((2 + other) * BLK, BLK), BLK)
    prev_row = pl.ds(pl.multiple_of(core * BLK, BLK), BLK)
    loads = [
        (decay_hbm, decay_v), (step_hbm, step_v), (k_hbm, k_stage), (v_hbm, v_stage),
        (k_hbm.at[core], k_win.at[mine]), (v_hbm.at[core], v_win.at[mine]),
        (q_hbm.at[core], q_span.at[core]),
        (b_hbm, b_v), (c_hbm, c_v), (gain_hbm, gain_v),
    ]
    loads = [pltpu.make_async_copy(s, d, load_sem.at[i]) for i, (s, d) in enumerate(loads)]
    for copy in loads:
        copy.start()

    barrier = pltpu.get_barrier_semaphore()

    def greet(device):
        pl.semaphore_signal(barrier, inc=1, device_id=device, device_id_type=MESH)

    def plane_device(index):
        return (z, index // (NY * NC), (index // NC) % NY, index % NC, hg)

    def z_device(index):
        return (index, x, y, core, hg)

    def ring(act):
        def visit(r, carry):
            act((me + r) % PLANE)
            return carry

        lax.fori_loop(1, PLANE, visit, 0)

    def each(low, high, act):
        def visit(n, carry):
            act(n)
            return carry

        lax.fori_loop(low, high, visit, 0)

    greet((bz, bx, by, 0, hg))
    greet((bz, bx, by, 1, hg))
    ring(lambda n: greet(plane_device(n)))
    for r in range(1, NH):
        greet((z, p_from[1], p_from[2], p_from[3], (hg + r) % NH))

    @pl.when(jnp.logical_and(z_moves, from_z > z))
    def _():
        greet(z_from)

    @pl.when(jnp.logical_and(z_moves, to_z > z))
    def _():
        greet(z_to)

    @pl.when(jnp.logical_and(relaying, core == 0))
    def _():
        greet(relay_from)
        greet(relay_to)

    each(z + 1, NZ, lambda n: greet(z_device(n)))

    loads[0].wait()
    loads[1].wait()
    row = lax.broadcasted_iota(jnp.int32, (SPAN, SPAN), 0)
    col = lax.broadcasted_iota(jnp.int32, (SPAN, SPAN), 1)
    causal = row <= col
    cum = dot(decay_v[...], causal.astype(F32), ((1,), (0,)), precision=lax.Precision.HIGHEST)
    total = cum[:, SPAN - 1:]
    tail = jnp.exp(total - cum) * step_v[...]
    shift = jnp.log(step_v[...]) - cum
    for k in range(16):
        cum_v[k] = jnp.broadcast_to(cum[k:k + 1], (8, SPAN))
        w_v[k] = jnp.broadcast_to(tail[k:k + 1], (8, SPAN))
        v_v[k] = jnp.broadcast_to(shift[k:k + 1], (8, SPAN))
    for o in range(8):
        lines = [total[8 * (n % 2) + o:8 * (n % 2) + o + 1] for n in range(8)]
        tot_out[o] = jnp.broadcast_to(jnp.concatenate(lines, 0), (8, 128))
    for copy in loads[2:]:
        copy.wait()

    @pl.when(span == 0)
    def _():
        k_win[:2 * BLK] = jnp.zeros((2 * BLK, 256), BF16)
        v_win[:2 * BLK] = jnp.zeros((2 * BLK, 256), BF16)

    def one(condition):
        return jnp.where(condition, 1, 0)

    greeted = (
        z + one(jnp.logical_and(z_moves, to_z < z)) + one(jnp.logical_and(z_moves, from_z < z))
        + 2 * one(jnp.logical_and(relaying, core == 1))
    )
    pl.semaphore_wait(barrier, NC + PLANE - 1 + NH - 1 + greeted)

    def reply(semaphore, device):
        pl.semaphore_signal(semaphore, inc=1, device_id=device, device_id_type=MESH)

    each(0, z, lambda n: reply(later_sem, z_device(n)))

    @pl.when(jnp.logical_and(z_moves, from_z < z))
    def _():
        reply(ready_sem, z_from)

    @pl.when(jnp.logical_and(relaying, core == 1))
    def _():
        reply(ready_sem, relay_from)

    def remote(src, dst, send, recv, to):
        return pltpu.make_async_remote_copy(
            src_ref=src, dst_ref=dst, send_sem=send, recv_sem=recv,
            device_id=to, device_id_type=MESH,
        )

    def cols(g, width=HDIM):
        return pl.ds(g * width, width)

    def halo(i, g, slot):
        stage, window = ((k_stage, k_win), (v_stage, v_win))[i]
        to = (az, ax, ay, jnp.where(wraps == 1, 1 - slot, slot), hg)
        return remote(
            stage.at[slot, :, cols(g)], window.at[prev_row, cols(g)],
            halo_send.at[i, g, slot], halo_recv.at[i, g, core], to,
        )

    def halo_arrival(i, g, block):
        part = (k_win, v_win)[i].at[pl.ds(block * BLK, BLK), cols(g)]
        return remote(part, part, halo_send.at[i, g, 0], halo_recv.at[i, g, block], partner)

    def swap(i, g):
        stage, window = ((k_stage, k_win), (v_stage, v_win))[i]
        return remote(
            stage.at[other, :, cols(g)], window.at[mine, cols(g)],
            swap_send.at[i, g], swap_recv.at[i, g], partner,
        )

    def swap_arrival(i, g):
        part = (k_win, v_win)[i].at[theirs, cols(g)]
        return remote(part, part, swap_send.at[i, g], swap_recv.at[i, g], partner)

    def q_swap(g):
        return remote(
            q_hbm.at[other, :, cols(g, 512)], q_span.at[core, :, cols(g, 512)],
            q_send.at[g], q_recv.at[g], partner,
        )

    def q_arrival(g):
        part = q_span.at[other, :, cols(g, 512)]
        return remote(part, part, q_send.at[g], q_recv.at[g], partner)

    last_chip = chip == CHIPS - 1
    for g in range(2):
        for i in range(2):
            halo(i, g, 0).start()
            pl.when(jnp.logical_not(last_chip))(halo(i, g, 1).start)
        q_swap(g).start()
        for i in range(2):
            swap(i, g).start()

    def tot_copy(to):
        return remote(
            tot_out.at[to // 2], tot_in.at[me], tot_send.at[0], tot_recv.at[0], plane_device(to)
        )

    ring(lambda to: tot_copy(to).start())
    tot_in[me] = tot_out[me // 2]
    for p in range(8):
        line = jnp.broadcast_to(gain_v[p:p + 1, :], (BLK, BLK))
        gcol[p * BLK:(p + 1) * BLK, :] = jnp.transpose(line)

    scale = math.log2(math.e) / math.sqrt(HDIM)
    j = lax.broadcasted_iota(jnp.int32, (3 * BLK, 4 * BLK), 0)
    i = lax.broadcasted_iota(jnp.int32, (3 * BLK, 4 * BLK), 1) % BLK
    first = one(span == 0)

    def part(q):
        return pl.ds(q * WIDE, WIDE)

    def z_copy(q):
        return remote(
            att.at[part(q)], z_in.at[long_out, part(q)], z_send.at[q], z_recv.at[long_out, q], z_to
        )

    def z_keep(q):
        return pltpu.make_async_copy(att.at[part(q)], z_in.at[0, part(q)], z_recv.at[0, q])

    def relay_copy(q):
        return remote(
            z_in.at[1, part(q)], z_in.at[0, part(q)], relay_send.at[q], z_recv.at[0, q], relay_to
        )

    def z_arrival(at, q):
        return remote(
            z_in.at[at, part(q)], z_in.at[at, part(q)], relay_send.at[q], z_recv.at[at, q], relay_to
        )

    def p_copy(q):
        return remote(z_in.at[0, part(q)], att_in.at[part(q)], att_send.at[q], att_recv.at[q], p_to)

    def p_keep(q):
        return pltpu.make_async_copy(z_in.at[0, part(q)], att_in.at[part(q)], att_recv.at[q])

    def either(here, keep, leave):
        pl.when(here)(keep)
        pl.when(jnp.logical_not(here))(leave)

    def sqz_copy():
        return remote(sq_out, sq_mid.at[long_out], sqz_send.at[0], sqz_recv.at[long_out], z_to)

    def sqz_keep():
        return pltpu.make_async_copy(sq_out, sq_mid.at[0], sqz_recv.at[0])

    def sqr_copy():
        return remote(sq_mid.at[1], sq_mid.at[0], sqr_send.at[0], sqz_recv.at[0], relay_to)

    def sqz_arrival(at):
        return remote(sq_mid.at[at], sq_mid.at[at], sqr_send.at[0], sqz_recv.at[at], relay_to)

    def sq_copy(to, at):
        return remote(
            sq_mid.at[0], sq_in.at[at], sq_send.at[to], sq_recv.at[at],
            (z, p_to[1], p_to[2], p_to[3], to),
        )

    def sq_keep():
        return pltpu.make_async_copy(sq_mid.at[0], sq_in.at[hg], sq_recv.at[hg])

    sums = [jnp.zeros((1, BLK), F32) for _ in range(2)]
    for g in range(2):
        @pl.when(span > 0)
        def _():
            for t in range(2):
                for block in range(2):
                    halo_arrival(t, g, block).wait_recv()

        for t in range(2):
            swap_arrival(t, g).wait_recv()
        q_arrival(g).wait_recv()
        lanes = slice(g * HDIM, (g + 1) * HDIM)
        for a in range(2):
            keys = k_win[a * BLK:(a + 3) * BLK, lanes]
            vals = jnp.transpose(v_win[a * BLK:(a + 3) * BLK, lanes])
            heads = [q_span[a, :, (4 * g + h) * HDIM:(4 * g + h + 1) * HDIM] for h in range(4)]
            score = dot(keys, jnp.concatenate(heads, 0), ((1,), (1,)))
            low = jnp.maximum(i + 1, first * (2 - a) * BLK)
            allowed = (j >= low) & (j <= i + 2 * BLK)
            score = jnp.where(allowed, score, -jnp.inf)
            peak = jnp.max(score, axis=0, keepdims=True)
            terms = jnp.exp2((score - peak) * scale)
            sum_terms = jnp.sum(terms, axis=0, keepdims=True)
            got = dot(vals, terms.astype(BF16), ((1,), (0,)))
            got = (got * (1.0 / sum_terms)).astype(BF16)
            for h in range(4):
                head = got[:, h * BLK:(h + 1) * BLK]
                att[(4 * g + h) * HDIM:(4 * g + h + 1) * HDIM, a * BLK:(a + 1) * BLK] = head
                wide = head.astype(F32)
                sums[a] = sums[a] + jnp.sum(wide * wide, axis=0, keepdims=True)
        if g == 0:
            @pl.when(jnp.logical_and(z_moves, to_z > z))
            def _():
                pl.semaphore_wait(ready_sem, 1)
        else:
            sq_out[...] = jnp.broadcast_to(jnp.concatenate(sums, 1), (8, SPAN))
            either(z_stays, lambda: sqz_keep().start(), lambda: sqz_copy().start())
        for q in (2 * g, 2 * g + 1):
            either(z_stays, z_keep(q).start, z_copy(q).start)

    cross = dot(b_v[...], c_v[...], ((1,), (1,)))

    def make_mix(k, carry):
        ct = cum_v[k, 0:1, :]
        for ub in range(2):
            line = v_v[k, 0:1, ub * BLK:(ub + 1) * BLK]
            colb = jnp.transpose(jnp.broadcast_to(line, (BLK, BLK)))
            arg = ct + jnp.concatenate([colb, colb], 1)
            rows = slice(ub * BLK, (ub + 1) * BLK)
            arg = jnp.where(causal[rows], arg, -jnp.inf)
            mix[k, rows] = (jnp.exp(arg) * cross[rows]).astype(BF16)
        return carry

    lax.fori_loop(0, 16, make_mix, 0)

    def make_ecum(p, carry):
        lanes = pl.ds(pl.multiple_of(p * BLK, BLK), BLK)
        for tb in range(2):
            half = slice(tb * BLK, (tb + 1) * BLK)
            pair = [
                jnp.broadcast_to(jnp.exp(cum_v[2 * p + h, 0:1, half]), (SDIM, BLK))
                for h in range(2)
            ]
            ecum[half, lanes] = jnp.transpose(jnp.concatenate(pair, 0))
        return carry

    lax.fori_loop(0, 8, make_ecum, 0)

    @pl.when(jnp.logical_and(relaying, core == 0))
    def _():
        pl.semaphore_wait(ready_sem, 1)

    def arrive(q):
        @pl.when(relaying)
        def _():
            z_arrival(1, q).wait_recv()
            relay_copy(q).start()

        either(z_stays, z_keep(q).wait, z_arrival(0, q).wait_recv)
        either(p_stays, p_keep(q).start, p_copy(q).start)

    def arrive_squares():
        @pl.when(relaying)
        def _():
            sqz_arrival(1).wait_recv()
            sqr_copy().start()

        either(z_stays, lambda: sqz_keep().wait(), lambda: sqz_arrival(0).wait_recv())
        for r in range(1, NH):
            sq_copy((hg + r) % NH, hg).start()
        either(p_stays, lambda: sq_keep().start(), lambda: sq_copy(hg, hg).start())

    def st_copy(q, to):
        return remote(
            st_out.at[q, to], st_in.at[q, me], st_send.at[q], st_recv.at[q], plane_device(to)
        )

    def run_copy(q, to, at):
        return remote(
            run_out.at[q], run_in.at[q, at], run_send.at[q, to], run_recv.at[q, at], z_device(to)
        )

    def log_copy(to, at):
        return remote(plane_out, plane_in.at[at], log_send.at[to], log_recv.at[at], z_device(to))

    def en_copy(q, to):
        return remote(
            en_out.at[q, to], en_in.at[q, me], en_send.at[q], en_recv.at[q], plane_device(to)
        )

    def sent(buffer, semaphore):
        rest = buffer.at[pl.ds(0, PLANE - 1)]
        return remote(rest, rest, semaphore, semaphore, partner)

    def states(q):
        if q == 0:
            for r in range(1, NH):
                sq_copy((hg + r) % NH, (hg + r) % NH).wait_recv()
            either(p_stays, lambda: sq_keep().wait(), lambda: sq_copy(hg, hg).wait_recv())
        for c in (2 * q, 2 * q + 1):
            either(p_stays, p_keep(c).wait, p_copy(c).wait_recv)
        square = sq_in[0] + sq_in[1] + sq_in[2] + sq_in[3]
        rate = lax.rsqrt(square[0:1] / FEATS + 1e-06)

        def make_normed(k, carry):
            rows = pl.ds(pl.multiple_of(k * SDIM, SDIM), SDIM)
            gain = gcol[rows, :]
            value = att_in[rows, :].astype(F32) * jnp.concatenate([gain, gain], 1) * rate
            value = value.astype(BF16)
            normed[rows, :] = value
            weighted[rows, :] = (value.astype(F32) * w_v[k, 0:1, :]).astype(BF16)
            return carry

        lax.fori_loop(8 * q, 8 * q + 8, make_normed, 0)
        state = dot(weighted[q * HALF:(q + 1) * HALF], b_v[...], ((1,), (0,)))
        st_out[q] = state.astype(BF16).reshape(PLANE, SLICE, STATE)
        ring(lambda to: st_copy(q, to).start())
        st_in[q, me] = st_out[q, me]

    def locals_(q):
        def make_local(p, carry):
            lanes = pl.ds(pl.multiple_of(p * BLK, BLK), BLK)
            pair = []
            for h in range(2):
                k = 2 * p + h
                rows = pl.ds(pl.multiple_of(k * SDIM, SDIM), SDIM)
                value = normed[rows, :]
                pair.append(dot(value, mix[k], ((1,), (0,))) + value.astype(F32) * skip_ref[k])
            both = jnp.concatenate(pair, 0)
            for tb in range(2):
                half = slice(tb * BLK, (tb + 1) * BLK)
                local[half, lanes] = jnp.transpose(both[:, half])
            return carry

        lax.fori_loop(4 * q, 4 * q + 4, make_local, 0)

    def prefix(q):
        sent(st_in.at[q], st_recv.at[q]).wait_recv()
        running = jnp.zeros((SLICE, STATE), F32)
        for n in range(PLANE):
            pre_v[q, n] = running
            running = decays[n, q:q + 1] * running + st_in[q, n].astype(F32)
        run_out[q] = running.astype(BF16)
        each(z + 1, NZ, lambda to: run_copy(q, to, z).start())

    def enter(q):
        if q == 0:
            each(0, z, lambda n: log_copy(n, n).wait_recv())

        def gather(n, carried):
            run_copy(q, n, n).wait_recv()
            decay = jnp.exp(plane_in[n])
            return decay[q:q + 1] * carried + run_in[q, n].astype(F32)

        carried = lax.fori_loop(0, z, gather, jnp.zeros((SLICE, STATE), F32))
        for n in range(PLANE):
            en_out[q, n] = (pre_v[q, n] + starts[n, q:q + 1] * carried).astype(BF16)
        ring(lambda to: en_copy(q, to).start())
        en_in[q, me] = en_out[q, me]

    def finish(q):
        sent(en_in.at[q], en_recv.at[q]).wait_recv()
        lanes = slice(q * HALF, (q + 1) * HALF)
        entry = dot(c_v[...], en_in[q].reshape(HALF, STATE), ((1,), (1,)))
        out_ref[:, lanes] = (local[:, lanes] + ecum[:, lanes] * entry).astype(BF16)

    arrive(0)
    arrive(1)
    arrive_squares()

    sent(tot_in, tot_recv.at[0]).wait_recv()
    logs = jnp.zeros((8, 128), F32)
    for n in range(PLANE):
        starts[n] = jnp.exp(logs)
        decays[n] = jnp.exp(tot_in[n])
        logs = logs + tot_in[n]
    plane_out[...] = logs

    @pl.when(z < NZ - 1)
    def _():
        pl.semaphore_wait(later_sem, NZ - 1 - z)

    each(z + 1, NZ, lambda to: log_copy(to, z).start())
    states(0)
    arrive(2)
    arrive(3)
    locals_(0)
    states(1)
    locals_(1)
    for stage in (prefix, enter, finish):
        for q in range(HALVES):
            stage(q)

    for g in range(2):
        for t in range(2):
            halo(t, g, 0).wait_send()
            pl.when(jnp.logical_not(last_chip))(halo(t, g, 1).wait_send)
            swap(t, g).wait_send()
        q_swap(g).wait_send()
    for r in range(1, NH):
        sq_copy((hg + r) % NH, hg).wait_send()

    @pl.when(z_moves)
    def _():
        sqz_copy().wait_send()
        for q in range(CHUNKS):
            z_copy(q).wait_send()

    @pl.when(relaying)
    def _():
        sqr_copy().wait_send()
        for q in range(CHUNKS):
            relay_copy(q).wait_send()

    @pl.when(p_moves)
    def _():
        sq_copy(hg, hg).wait_send()
        for q in range(CHUNKS):
            p_copy(q).wait_send()

    sent(tot_in, tot_send.at[0]).wait_send()
    each(z + 1, NZ, lambda to: log_copy(to, z).wait_send())
    for q in range(HALVES):
        sent(st_out.at[q], st_send.at[q]).wait_send()
        each(z + 1, NZ, lambda to: run_copy(q, to, z).wait_send())
        sent(en_out.at[q], en_send.at[q]).wait_send()


def body(query, keys, values, norm_gain, in_b, out_c, step, log_decay, skip):
    feats = query.shape[2]
    gain = norm_gain.reshape(feats // HDIM, HDIM)
    dma = pltpu.SemaphoreType.DMA
    vm = pltpu.VMEM
    scratch = [
        vm((2, BLK, feats), BF16),
        vm((2, BLK, 256), BF16),
        vm((2, BLK, 256), BF16),
        vm((4 * BLK, 256), BF16),
        vm((4 * BLK, 256), BF16),
        vm((8, HDIM), F32),
        vm((SPAN, STATE), BF16),
        vm((SPAN, STATE), BF16),
        vm((16, SPAN), F32),
        vm((16, SPAN), F32),
        vm((16, 8, SPAN), F32),
        vm((16, 8, SPAN), F32),
        vm((16, 8, SPAN), F32),
        vm((feats, 128), F32),
        vm((16, SPAN, SPAN), BF16),
        vm((SPAN, feats), F32),
        vm((feats, SPAN), BF16),
        vm((2, feats, SPAN), BF16),
        vm((feats, SPAN), BF16),
        vm((8, SPAN), F32),
        vm((2, 8, SPAN), F32),
        vm((NH, 8, SPAN), F32),
        vm((feats, SPAN), BF16),
        vm((feats, SPAN), BF16),
        vm((SPAN, feats), F32),
        vm((8, 8, 128), F32),
        vm((PLANE, 8, 128), F32),
        vm((PLANE, 8, 128), F32),
        vm((PLANE, 8, 128), F32),
        vm((8, 128), F32),
        vm((NZ, 8, 128), F32),
        vm((HALVES, PLANE, SLICE, STATE), BF16),
        vm((HALVES, PLANE, SLICE, STATE), BF16),
        vm((HALVES, PLANE, SLICE, STATE), F32),
        vm((HALVES, SLICE, STATE), BF16),
        vm((HALVES, NZ, SLICE, STATE), BF16),
        vm((HALVES, PLANE, SLICE, STATE), BF16),
        vm((HALVES, PLANE, SLICE, STATE), BF16),
        dma((10,)),
        dma((2, 2, 2)), dma((2, 2, 2)),
        dma((2, 2)), dma((2, 2)),
        dma((2,)), dma((2,)),
        dma((CHUNKS,)), dma((2, CHUNKS)),
        dma((CHUNKS,)),
        dma((CHUNKS,)), dma((CHUNKS,)),
        dma((1,)), dma((2,)), dma((1,)),
        dma((NH,)), dma((NH,)),
        dma((1,)), dma((1,)),
        dma((NZ,)), dma((NZ,)),
        dma((HALVES,)), dma((HALVES,)),
        dma((HALVES, NZ)), dma((HALVES, NZ)),
        dma((HALVES,)), dma((HALVES,)),
        pltpu.SemaphoreType.REGULAR,
        pltpu.SemaphoreType.REGULAR,
    ]
    anywhere = pl.BlockSpec(memory_space=pl.ANY)
    return pl.pallas_call(
        kernel,
        out_shape=jax.ShapeDtypeStruct((SPAN, feats), BF16),
        in_specs=[anywhere] * 8 + [pl.BlockSpec(memory_space=pltpu.SMEM)],
        out_specs=pl.BlockSpec(memory_space=pltpu.VMEM),
        scratch_shapes=scratch,
        compiler_params=pltpu.CompilerParams(collective_id=0, has_side_effects=True),
    )(query, keys, values, gain, in_b, out_c, step, log_decay, skip)


def solution(mesh):
    torus = Mesh(mesh.devices.reshape(NZ, NX, NY, NC, NH), AXES)
    return jax.shard_map(
        body,
        mesh=torus,
        in_specs=(
            P(None, SEQ, "head"),
            P(None, SEQ, "head"),
            P(None, SEQ, "head"),
            P("head"),
            P(SEQ, None),
            P(SEQ, None),
            P("head", SEQ),
            P("head", SEQ),
            P("head"),
        ),
        out_specs=P(SEQ, "head"),
        check_vma=False,
    )
```

time: 93 us -> 68.7 us (0.74)
  the two profiles are of different devices: /device:TPU:1 before, /device:TPU:129 now
where the time goes in v3:
time: 68.7 us; the launch traced here: 68.5 us
  Pallas kernels  66.6 us (97%)
  local copies, waits for them, and re-layouts  1.87 us (3%)
    pallas_call x1, Pallas kernels, body(): pl.pallas_call(kernel, out_shape=jax.ShapeDtypeStruct((SPAN, feats), BF16...  66.6 us
    unnamed x1, local copies, waits for them, and re-layouts  1.87 us

profile of v3, /device:TPU:129, one launch (start us, length us, event | category | flops | bytes accessed | tf_op | source)
XLA Modules:
  0.0 68.5 jit_solution(8332029577094914583)
XLA Ops:
  0.0 66.6 %shard_map.91 = bf16[256,1024]{1,0:T(8,128)(2,1)} custom-call(bf16[2,128,1024]{2,1,0:T(8,128)(2,1)} %q_hbm.1, bf16[2,128,256]{2,1,0:T(8,128)(2,1)} %k_hbm.1, bf16[2,128,256]{2,1,0:T(8,128)(2,1)} %v_hbm.1, f32[8,128]{1,0:T(8,128)} %bitcast.1, bf16[256,128]{1,0:T(8,128)(2,1)} %b_hbm.1, bf16[256,128]{1,0:T(8,128)(2,1)} %c_hbm.1, f32[16,256]{1,0:T(8,128)} %step_hbm.1, ...), custom_call_target="tpu_custom_call" | custom-call | tf_op jit(solution)/shard_map/pallas_call | solution.py:624
  66.6 1.9 %copy.11 = bf16[256,1024]{1,0:T(8,128)(2,1)} copy(bf16[256,1024]{1,0:T(8,128)(2,1)} %shard_map.91) | data formatting | bytes 1048576

commit v4 on v3

--- a/solution.py
+++ b/solution.py
@@ -45,13 +45,14 @@
     q_hbm, k_hbm, v_hbm, gain_hbm, b_hbm, c_hbm, step_hbm, decay_hbm, skip_ref,
     out_ref,
     q_span, k_stage, v_stage, k_win, v_win, gain_v, b_v, c_v, step_v, decay_v,
-    cum_v, w_v, v_v, gcol, mix, ecum, att, z_in, att_in, sq_out, sq_mid, sq_in, normed, weighted, local,
-    tot_out, tot_in, decays, starts, plane_out, plane_in,
-    st_out, st_in, pre_v, run_out, run_in, en_out, en_in,
+    cum_v, v_v, gcol, mix, ecum, att, z_in, att_in, sq_out, sq_mid, sq_in, sq_here, weighted, local,
+    w_out, w_here, b_here, tot_here, tot_out, tot_in, run_tot, starts, plane_out, plane_in,
+    st_out, st_in, pre_out, pre_in, run_out, run_in, en_out, en_in,
     load_sem, halo_send, halo_recv, swap_send, swap_recv, q_send, q_recv, z_send, z_recv,
     relay_send, att_send, att_recv, sqz_send, sqz_recv, sqr_send, sq_send, sq_recv,
+    here_send, here_recv, home_send, home_recv, vtot_send, vtot_recv, pre_send, pre_recv,
     tot_send, tot_recv, log_send, log_recv, st_send, st_recv, run_send, run_recv,
-    en_send, en_recv, ready_sem, later_sem,
+    en_send, en_recv, ready_sem, later_sem, home_ready,
 ):
     z, x, y, core, hg = (lax.axis_index(a) for a in AXES)
     chip = (z * NX + x) * NY + y
@@ -87,6 +88,13 @@
     p_stays = jnp.logical_and(p_to[1] == x, jnp.logical_and(p_to[2] == y, p_to[3] == core))
     p_moves = jnp.logical_not(p_stays)
 
+    seq = z * PLANE + me
+    fz, fx, fy, fc = seq_coords(span)
+    home = (fz, fx, fy, fc, hg)
+    sz, sx, sy = chip_coords(seq % CHIPS)
+    away = (sz, sx, sy, seq // CHIPS, hg)
+    stays = span == seq
+
     mine = pl.ds(pl.multiple_of((2 + core) * BLK, BLK), BLK)
     theirs = pl.ds(pl.multiple_of((2 + other) * BLK, BLK), BLK)
     prev_row = pl.ds(pl.multiple_of(core * BLK, BLK), BLK)
@@ -145,6 +153,16 @@
         greet(relay_to)
 
     each(z + 1, NZ, lambda n: greet(z_device(n)))
+    for r in range(1, NH):
+        greet((z, x, y, core, (hg + r) % NH))
+
+    @pl.when(fz > z)
+    def _():
+        greet(home)
+
+    @pl.when(sz > z)
+    def _():
+        greet(away)
 
     loads[0].wait()
     loads[1].wait()
@@ -153,11 +171,10 @@
     causal = row <= col
     cum = dot(decay_v[...], causal.astype(F32), ((1,), (0,)), precision=lax.Precision.HIGHEST)
     total = cum[:, SPAN - 1:]
-    tail = jnp.exp(total - cum) * step_v[...]
+    w_out[...] = jnp.exp(total - cum) * step_v[...]
     shift = jnp.log(step_v[...]) - cum
     for k in range(16):
         cum_v[k] = jnp.broadcast_to(cum[k:k + 1], (8, SPAN))
-        w_v[k] = jnp.broadcast_to(tail[k:k + 1], (8, SPAN))
         v_v[k] = jnp.broadcast_to(shift[k:k + 1], (8, SPAN))
     for o in range(8):
         lines = [total[8 * (n % 2) + o:8 * (n % 2) + o + 1] for n in range(8)]
@@ -175,9 +192,9 @@
 
     greeted = (
         z + one(jnp.logical_and(z_moves, to_z < z)) + one(jnp.logical_and(z_moves, from_z < z))
-        + 2 * one(jnp.logical_and(relaying, core == 1))
+        + 2 * one(jnp.logical_and(relaying, core == 1)) + one(sz < z) + one(fz < z)
     )
-    pl.semaphore_wait(barrier, NC + PLANE - 1 + NH - 1 + greeted)
+    pl.semaphore_wait(barrier, NC + PLANE - 1 + 2 * (NH - 1) + greeted)
 
     def reply(semaphore, device):
         pl.semaphore_signal(semaphore, inc=1, device_id=device, device_id_type=MESH)
@@ -191,6 +208,10 @@
     @pl.when(jnp.logical_and(relaying, core == 1))
     def _():
         reply(ready_sem, relay_from)
+
+    @pl.when(fz < z)
+    def _():
+        reply(home_ready, home)
 
     def remote(src, dst, send, recv, to):
         return pltpu.make_async_remote_copy(
@@ -310,6 +331,26 @@
 
     def sq_keep():
         return pltpu.make_async_copy(sq_mid.at[0], sq_in.at[hg], sq_recv.at[hg])
+
+    home_pairs = ((b_v, b_here), (w_out, w_here), (tot_out, tot_here))
+
+    def home_copy(n):
+        return remote(
+            home_pairs[n][0], home_pairs[n][1], home_send.at[n], home_recv.at[n], away
+        )
+
+    def home_keep(n):
+        return pltpu.make_async_copy(home_pairs[n][0], home_pairs[n][1], home_recv.at[n])
+
+    def here_copy(r):
+        return remote(
+            sq_out, sq_here.at[hg], here_send.at[r], here_recv.at[hg],
+            (z, x, y, core, (hg + r) % NH),
+        )
+
+    def here_arrival(r):
+        n = (hg + r) % NH
+        return remote(sq_here.at[n], sq_here.at[n], here_send.at[r], here_recv.at[n], partner)
 
     sums = [jnp.zeros((1, BLK), F32) for _ in range(2)]
     for g in range(2):
@@ -347,9 +388,19 @@
                 pl.semaphore_wait(ready_sem, 1)
         else:
             sq_out[...] = jnp.broadcast_to(jnp.concatenate(sums, 1), (8, SPAN))
+            for r in range(1, NH):
+                here_copy(r).start()
+            sq_here[hg] = sq_out[...]
             either(z_stays, lambda: sqz_keep().start(), lambda: sqz_copy().start())
         for q in (2 * g, 2 * g + 1):
             either(z_stays, z_keep(q).start, z_copy(q).start)
+        if g == 0:
+            @pl.when(sz > z)
+            def _():
+                pl.semaphore_wait(home_ready, 1)
+
+            for n in range(3):
+                either(stays, home_keep(n).start, home_copy(n).start)
 
     cross = dot(b_v[...], c_v[...], ((1,), (1,)))
 
@@ -408,10 +459,43 @@
             st_out.at[q, to], st_in.at[q, me], st_send.at[q], st_recv.at[q], plane_device(to)
         )
 
-    def run_copy(q, to, at):
-        return remote(
-            run_out.at[q], run_in.at[q, at], run_send.at[q, to], run_recv.at[q, at], z_device(to)
-        )
+    def vtot_copy(to):
+        return remote(
+            tot_here.at[to // 2], run_tot.at[me], vtot_send.at[0], vtot_recv.at[0],
+            plane_device(to),
+        )
+
+    def pre_copy(q, s):
+        return remote(
+            pre_out.at[q, s], pre_in.at[q, z % 2], pre_send.at[q, s], pre_recv.at[q, z % 2],
+            z_device(NZ // 2 * s + z // 2),
+        )
+
+    def pre_arrival(q, n):
+        return remote(
+            pre_in.at[q, n], pre_in.at[q, n], pre_send.at[q, 0], pre_recv.at[q, n], partner
+        )
+
+    def run_copy(q, s, to):
+        return remote(
+            run_out.at[q, s], run_in.at[q, NZ * s + z], run_send.at[q, s, to],
+            run_recv.at[q, NZ * s + z], z_device(to),
+        )
+
+    def run_arrival(q, n):
+        return remote(
+            run_in.at[q, n], run_in.at[q, n], run_send.at[q, 0, 0], run_recv.at[q, n], partner
+        )
+
+    def run_targets(s, act):
+        @pl.when(jnp.logical_and(NZ // 2 * s + z // 2 != z, z % 2 == 0))
+        def _():
+            act(NZ // 2 * s + z // 2)
+
+        def visit(n):
+            pl.when(n != z)(lambda: act(n))
+
+        each(NZ // 2 * s + z // 2 + 1, NZ, visit)
 
     def log_copy(to, at):
         return remote(plane_out, plane_in.at[at], log_send.at[to], log_recv.at[at], z_device(to))
@@ -426,6 +510,20 @@
         return remote(rest, rest, semaphore, semaphore, partner)
 
     def states(q):
+        square = sq_here[0] + sq_here[1] + sq_here[2] + sq_here[3]
+        rate = lax.rsqrt(square[0:1] / FEATS + 1e-06)
+        for k in range(8 * q, 8 * q + 8):
+            rows = slice(k * SDIM, (k + 1) * SDIM)
+            gain = gcol[rows, :]
+            value = att[rows, :].astype(F32) * jnp.concatenate([gain, gain], 1) * rate
+            value = value.astype(BF16).astype(F32)
+            weighted[rows, :] = (value * w_here[k:k + 1, :]).astype(BF16)
+        state = dot(weighted[q * HALF:(q + 1) * HALF], b_here[...], ((1,), (0,)))
+        st_out[q] = state.astype(BF16).reshape(PLANE, SLICE, STATE)
+        ring(lambda to: st_copy(q, to).start())
+        st_in[q, me] = st_out[q, me]
+
+    def locals_(q):
         if q == 0:
             for r in range(1, NH):
                 sq_copy((hg + r) % NH, (hg + r) % NH).wait_recv()
@@ -435,29 +533,15 @@
         square = sq_in[0] + sq_in[1] + sq_in[2] + sq_in[3]
         rate = lax.rsqrt(square[0:1] / FEATS + 1e-06)
 
-        def make_normed(k, carry):
-            rows = pl.ds(pl.multiple_of(k * SDIM, SDIM), SDIM)
-            gain = gcol[rows, :]
-            value = att_in[rows, :].astype(F32) * jnp.concatenate([gain, gain], 1) * rate
-            value = value.astype(BF16)
-            normed[rows, :] = value
-            weighted[rows, :] = (value.astype(F32) * w_v[k, 0:1, :]).astype(BF16)
-            return carry
-
-        lax.fori_loop(8 * q, 8 * q + 8, make_normed, 0)
-        state = dot(weighted[q * HALF:(q + 1) * HALF], b_v[...], ((1,), (0,)))
-        st_out[q] = state.astype(BF16).reshape(PLANE, SLICE, STATE)
-        ring(lambda to: st_copy(q, to).start())
-        st_in[q, me] = st_out[q, me]
-
-    def locals_(q):
         def make_local(p, carry):
             lanes = pl.ds(pl.multiple_of(p * BLK, BLK), BLK)
             pair = []
             for h in range(2):
                 k = 2 * p + h
                 rows = pl.ds(pl.multiple_of(k * SDIM, SDIM), SDIM)
-                value = normed[rows, :]
+                gain = gcol[rows, :]
+                value = att_in[rows, :].astype(F32) * jnp.concatenate([gain, gain], 1) * rate
+                value = value.astype(BF16)
                 pair.append(dot(value, mix[k], ((1,), (0,))) + value.astype(F32) * skip_ref[k])
             both = jnp.concatenate(pair, 0)
             for tb in range(2):
@@ -469,25 +553,52 @@
 
     def prefix(q):
         sent(st_in.at[q], st_recv.at[q]).wait_recv()
-        running = jnp.zeros((SLICE, STATE), F32)
-        for n in range(PLANE):
-            pre_v[q, n] = running
-            running = decays[n, q:q + 1] * running + st_in[q, n].astype(F32)
-        run_out[q] = running.astype(BF16)
-        each(z + 1, NZ, lambda to: run_copy(q, to, z).start())
+        for s in range(2):
+            running = jnp.zeros((SLICE, STATE), F32)
+            for n in range(8):
+                pre_out[q, s, n] = running.astype(BF16)
+                decay = jnp.exp(run_tot[2 * n + s])
+                running = decay[q:q + 1] * running + st_in[q, 2 * n + s].astype(F32)
+            run_out[q, s] = running.astype(BF16)
+        for s in range(2):
+            run_targets(s, lambda to: run_copy(q, s, to).start())
+            run_in[q, NZ * s + z] = run_out[q, s]
+        for s in range(2):
+            own = NZ // 2 * s + z // 2 == z
+            pl.when(jnp.logical_not(own))(pre_copy(q, s).start)
+
+            @pl.when(own)
+            def _():
+                pre_in[q, s] = pre_out[q, s]
 
     def enter(q):
+        for n in range(2):
+            @pl.when(2 * (z % (NZ // 2)) + n != z)
+            def _():
+                pre_arrival(q, n).wait_recv()
+
         if q == 0:
             each(0, z, lambda n: log_copy(n, n).wait_recv())
 
-        def gather(n, carried):
-            run_copy(q, n, n).wait_recv()
-            decay = jnp.exp(plane_in[n])
-            return decay[q:q + 1] * carried + run_in[q, n].astype(F32)
+        def arrived(n):
+            pl.when(n % NZ != z)(run_arrival(q, n).wait_recv)
+
+        def gather(p, carried):
+            for n in range(2):
+                arrived(2 * p + n)
+                decay = jnp.exp(plane_in[p, n])
+                carried = decay[q:q + 1] * carried + run_in[q, 2 * p + n].astype(F32)
+            return carried
 
         carried = lax.fori_loop(0, z, gather, jnp.zeros((SLICE, STATE), F32))
-        for n in range(PLANE):
-            en_out[q, n] = (pre_v[q, n] + starts[n, q:q + 1] * carried).astype(BF16)
+        for n in range(8):
+            value = pre_in[q, 0, n].astype(F32) + starts[n, q:q + 1] * carried
+            en_out[q, n] = value.astype(BF16)
+        arrived(2 * z)
+        carried = jnp.exp(plane_out[0])[q:q + 1] * carried + run_in[q, 2 * z].astype(F32)
+        for n in range(8):
+            value = pre_in[q, 1, n].astype(F32) + starts[8 + n, q:q + 1] * carried
+            en_out[q, 8 + n] = value.astype(BF16)
         ring(lambda to: en_copy(q, to).start())
         en_in[q, me] = en_out[q, me]
 
@@ -497,32 +608,42 @@
         entry = dot(c_v[...], en_in[q].reshape(HALF, STATE), ((1,), (1,)))
         out_ref[:, lanes] = (local[:, lanes] + ecum[:, lanes] * entry).astype(BF16)
 
+    for n in range(3):
+        either(stays, home_keep(n).wait, home_copy(n).wait_recv)
+    ring(lambda to: vtot_copy(to).start())
+    run_tot[me] = tot_here[me // 2]
+    for r in range(1, NH):
+        here_arrival(r).wait_recv()
+    for q in range(HALVES):
+        states(q)
+
+    sent(tot_in, tot_recv.at[0]).wait_recv()
+    for r in range(2):
+        logs = jnp.zeros((8, 128), F32)
+        for n in range(8 * r, 8 * r + 8):
+            starts[n] = jnp.exp(logs)
+            logs = logs + tot_in[n]
+        plane_out[r] = logs
+
+    @pl.when(z < NZ - 1)
+    def _():
+        pl.semaphore_wait(later_sem, NZ - 1 - z)
+
+    each(z + 1, NZ, lambda to: log_copy(to, z).start())
     arrive(0)
+    sent(run_tot, vtot_recv.at[0]).wait_recv()
+    prefix(0)
+    prefix(1)
     arrive(1)
     arrive_squares()
-
-    sent(tot_in, tot_recv.at[0]).wait_recv()
-    logs = jnp.zeros((8, 128), F32)
-    for n in range(PLANE):
-        starts[n] = jnp.exp(logs)
-        decays[n] = jnp.exp(tot_in[n])
-        logs = logs + tot_in[n]
-    plane_out[...] = logs
-
-    @pl.when(z < NZ - 1)
-    def _():
-        pl.semaphore_wait(later_sem, NZ - 1 - z)
-
-    each(z + 1, NZ, lambda to: log_copy(to, z).start())
-    states(0)
     arrive(2)
+    locals_(0)
     arrive(3)
-    locals_(0)
-    states(1)
+    enter(0)
+    enter(1)
     locals_(1)
-    for stage in (prefix, enter, finish):
-        for q in range(HALVES):
-            stage(q)
+    finish(0)
+    finish(1)
 
     for g in range(2):
         for t in range(2):
@@ -552,10 +673,21 @@
             p_copy(q).wait_send()
 
     sent(tot_in, tot_send.at[0]).wait_send()
+    sent(run_tot, vtot_send.at[0]).wait_send()
     each(z + 1, NZ, lambda to: log_copy(to, z).wait_send())
+    for r in range(1, NH):
+        here_copy(r).wait_send()
+
+    @pl.when(jnp.logical_not(stays))
+    def _():
+        for n in range(3):
+            home_copy(n).wait_send()
+
     for q in range(HALVES):
         sent(st_out.at[q], st_send.at[q]).wait_send()
-        each(z + 1, NZ, lambda to: run_copy(q, to, z).wait_send())
+        for s in range(2):
+            run_targets(s, lambda to: run_copy(q, s, to).wait_send())
+            pl.when(NZ // 2 * s + z // 2 != z)(pre_copy(q, s).wait_send)
         sent(en_out.at[q], en_send.at[q]).wait_send()
 
 
@@ -577,7 +709,6 @@
         vm((16, SPAN), F32),
         vm((16, 8, SPAN), F32),
         vm((16, 8, SPAN), F32),
-        vm((16, 8, SPAN), F32),
         vm((feats, 128), F32),
         vm((16, SPAN, SPAN), BF16),
         vm((SPAN, feats), F32),
@@ -587,20 +718,25 @@
         vm((8, SPAN), F32),
         vm((2, 8, SPAN), F32),
         vm((NH, 8, SPAN), F32),
-        vm((feats, SPAN), BF16),
+        vm((NH, 8, SPAN), F32),
         vm((feats, SPAN), BF16),
         vm((SPAN, feats), F32),
+        vm((16, SPAN), F32),
+        vm((16, SPAN), F32),
+        vm((SPAN, STATE), BF16),
+        vm((8, 8, 128), F32),
         vm((8, 8, 128), F32),
         vm((PLANE, 8, 128), F32),
         vm((PLANE, 8, 128), F32),
         vm((PLANE, 8, 128), F32),
-        vm((8, 128), F32),
-        vm((NZ, 8, 128), F32),
+        vm((2, 8, 128), F32),
+        vm((NZ, 2, 8, 128), F32),
         vm((HALVES, PLANE, SLICE, STATE), BF16),
         vm((HALVES, PLANE, SLICE, STATE), BF16),
-        vm((HALVES, PLANE, SLICE, STATE), F32),
-        vm((HALVES, SLICE, STATE), BF16),
-        vm((HALVES, NZ, SLICE, STATE), BF16),
+        vm((HALVES, 2, 8, SLICE, STATE), BF16),
+        vm((HALVES, 2, 8, SLICE, STATE), BF16),
+        vm((HALVES, 2, SLICE, STATE), BF16),
+        vm((HALVES, 2 * NZ, SLICE, STATE), BF16),
         vm((HALVES, PLANE, SLICE, STATE), BF16),
         vm((HALVES, PLANE, SLICE, STATE), BF16),
         dma((10,)),
@@ -612,11 +748,16 @@
         dma((CHUNKS,)), dma((CHUNKS,)),
         dma((1,)), dma((2,)), dma((1,)),
         dma((NH,)), dma((NH,)),
+        dma((NH,)), dma((NH,)),
+        dma((3,)), dma((3,)),
+        dma((1,)), dma((1,)),
+        dma((HALVES, 2)), dma((HALVES, 2)),
         dma((1,)), dma((1,)),
         dma((NZ,)), dma((NZ,)),
         dma((HALVES,)), dma((HALVES,)),
-        dma((HALVES, NZ)), dma((HALVES, NZ)),
+        dma((HALVES, 2, NZ)), dma((HALVES, 2 * NZ)),
         dma((HALVES,)), dma((HALVES,)),
+        pltpu.SemaphoreType.REGULAR,
         pltpu.SemaphoreType.REGULAR,
         pltpu.SemaphoreType.REGULAR,
     ]

time: 68.7 us -> 79.9 us (1.16)
  the two profiles are of different devices: /device:TPU:129 before, /device:TPU:193 now
where the time goes in v4:
time: 79.9 us; the launch traced here: 79.7 us
  Pallas kernels  77.8 us (97%)
  local copies, waits for them, and re-layouts  1.87 us (2%)
    pallas_call x1, Pallas kernels, body(): pl.pallas_call(kernel, out_shape=jax.ShapeDtypeStruct((SPAN, feats), BF16...  77.8 us
    unnamed x1, local copies, waits for them, and re-layouts  1.87 us

profile of v4, /device:TPU:193, one launch (start us, length us, event | category | flops | bytes accessed | tf_op | source)
XLA Modules:
  0.0 79.7 jit_solution(15478494967410983956)
XLA Ops:
  0.0 77.8 %shard_map.91 = bf16[256,1024]{1,0:T(8,128)(2,1)} custom-call(bf16[2,128,1024]{2,1,0:T(8,128)(2,1)} %q_hbm.1, bf16[2,128,256]{2,1,0:T(8,128)(2,1)} %k_hbm.1, bf16[2,128,256]{2,1,0:T(8,128)(2,1)} %v_hbm.1, f32[8,128]{1,0:T(8,128)} %bitcast.1, bf16[256,128]{1,0:T(8,128)(2,1)} %b_hbm.1, bf16[256,128]{1,0:T(8,128)(2,1)} %c_hbm.1, f32[16,256]{1,0:T(8,128)} %step_hbm.1, ...), custom_call_target="tpu_custom_call" | custom-call | tf_op jit(solution)/shard_map/pallas_call | solution.py:765
  77.8 1.9 %copy.11 = bf16[256,1024]{1,0:T(8,128)(2,1)} copy(bf16[256,1024]{1,0:T(8,128)(2,1)} %shard_map.91) | data formatting | bytes 1048576

commit v5 on v4

--- a/solution.py
+++ b/solution.py
@@ -50,9 +50,9 @@
     st_out, st_in, pre_out, pre_in, run_out, run_in, en_out, en_in,
     load_sem, halo_send, halo_recv, swap_send, swap_recv, q_send, q_recv, z_send, z_recv,
     relay_send, att_send, att_recv, sqz_send, sqz_recv, sqr_send, sq_send, sq_recv,
-    here_send, here_recv, home_send, home_recv, vtot_send, vtot_recv, pre_send, pre_recv,
+    here_send, here_recv, home_send, home_recv, vtot_send, vtot_recv, pre_send, pre_recv, pre_on,
     tot_send, tot_recv, log_send, log_recv, st_send, st_recv, run_send, run_recv,
-    en_send, en_recv, ready_sem, later_sem, home_ready,
+    en_send, en_recv, ready_sem, later_sem, home_ready, head_sem,
 ):
     z, x, y, core, hg = (lax.axis_index(a) for a in AXES)
     chip = (z * NX + x) * NY + y
@@ -75,11 +75,21 @@
     to_z = jnp.where(long_out == 1, relay_of, NZ // 2 * core + z // 2)
     to_core = jnp.where(long_out == 1, core, z % 2)
     z_to = (to_z, x, y, to_core, hg)
+    long_half = jnp.where(z == jnp.where(core == 0, 5, 2), 1, 0)
+    helps = z == jnp.where(core == 0, 0, NZ - 1)
+    half_to = (
+        jnp.where(long_half == 1, jnp.where(core == 0, 0, NZ - 1), to_z), x, y,
+        jnp.where(long_half == 1, core, to_core), hg,
+    )
+    half_out = jnp.maximum(long_out, long_half)
     from_z = jnp.where(long_in == 1, jnp.where(core == 0, NZ - 2, 1), 2 * (z % (NZ // 2)) + core)
     from_core = jnp.where(long_in == 1, other, z // (NZ // 2))
     z_from = (from_z, x, y, from_core, hg)
     relay_from = (jnp.where(core == 0, NZ - 1, 0), x, y, core, hg)
-    relay_to = (jnp.where(core == 0, NZ // 2 - 1, NZ // 2), x, y, other, hg)
+    relay_z = jnp.where(
+        helps, jnp.where(core == 0, 2, 5), jnp.where(core == 0, NZ // 2 - 1, NZ // 2)
+    )
+    relay_to = (relay_z, x, y, other, hg)
     z_stays = jnp.logical_and(to_z == z, to_core == core)
     z_moves = jnp.logical_not(z_stays)
     relaying = relays == 1
@@ -136,8 +146,24 @@
     greet((bz, bx, by, 0, hg))
     greet((bz, bx, by, 1, hg))
     ring(lambda n: greet(plane_device(n)))
-    for r in range(1, NH):
-        greet((z, p_from[1], p_from[2], p_from[3], (hg + r) % NH))
+
+    def rank(h):
+        return jnp.where(h == 0, 0, jnp.where(h == 2, 2, 1))
+
+    level = rank(hg)
+    same = (z, x, y, core)
+
+    def to_heads(position, test, act):
+        for r in range(1, NH):
+            h = (hg + r) % NH
+
+            @pl.when(test(rank(h)))
+            def _():
+                act((*position, h))
+
+    to_heads(p_from[:4], lambda n: n >= level, greet)
+    to_heads(p_to[:4], lambda n: n > level, greet)
+    to_heads(same, lambda n: n >= level, greet)
 
     @pl.when(jnp.logical_and(z_moves, from_z > z))
     def _():
@@ -150,12 +176,16 @@
     @pl.when(jnp.logical_and(relaying, core == 0))
     def _():
         greet(relay_from)
+
+    @pl.when(jnp.logical_and(jnp.logical_or(relaying, helps), core == 0))
+    def _():
         greet(relay_to)
 
+    @pl.when(jnp.logical_and(z == 5, core == 0))
+    def _():
+        greet((NZ - 1, x, y, 1, hg))
+
     each(z + 1, NZ, lambda n: greet(z_device(n)))
-    for r in range(1, NH):
-        greet((z, x, y, core, (hg + r) % NH))
-
     @pl.when(fz > z)
     def _():
         greet(home)
@@ -193,13 +223,17 @@
     greeted = (
         z + one(jnp.logical_and(z_moves, to_z < z)) + one(jnp.logical_and(z_moves, from_z < z))
         + 2 * one(jnp.logical_and(relaying, core == 1)) + one(sz < z) + one(fz < z)
+        + one(jnp.logical_and(jnp.logical_or(z == 2, z == NZ - 1), core == 1))
     )
-    pl.semaphore_wait(barrier, NC + PLANE - 1 + 2 * (NH - 1) + greeted)
+    heads = jnp.where(level == 0, 0, jnp.where(level == 1, 5, 9))
+    pl.semaphore_wait(barrier, NC + PLANE - 1 + heads + greeted)
 
     def reply(semaphore, device):
         pl.semaphore_signal(semaphore, inc=1, device_id=device, device_id_type=MESH)
 
     each(0, z, lambda n: reply(later_sem, z_device(n)))
+    to_heads(p_from[:4], lambda n: n < level, lambda d: reply(head_sem, d))
+    to_heads(same, lambda n: n < level, lambda d: reply(head_sem, d))
 
     @pl.when(jnp.logical_and(z_moves, from_z < z))
     def _():
@@ -208,6 +242,10 @@
     @pl.when(jnp.logical_and(relaying, core == 1))
     def _():
         reply(ready_sem, relay_from)
+
+    @pl.when(jnp.logical_and(z == 2, core == 1))
+    def _():
+        reply(ready_sem, (0, x, y, 0, hg))
 
     @pl.when(fz < z)
     def _():
@@ -219,6 +257,10 @@
             device_id=to, device_id_type=MESH,
         )
 
+    def either(here, keep, leave):
+        pl.when(here)(keep)
+        pl.when(jnp.logical_not(here))(leave)
+
     def cols(g, width=HDIM):
         return pl.ds(g * width, width)
 
@@ -256,7 +298,21 @@
         return remote(part, part, q_send.at[g], q_recv.at[g], partner)
 
     last_chip = chip == CHIPS - 1
-    for g in range(2):
+    home_pairs = ((b_v, b_here), (w_out, w_here), (tot_out, tot_here))
+
+    def home_copy(n):
+        return remote(
+            home_pairs[n][0], home_pairs[n][1], home_send.at[n], home_recv.at[n], away
+        )
+
+    def home_keep(n):
+        return pltpu.make_async_copy(home_pairs[n][0], home_pairs[n][1], home_recv.at[n])
+
+    def send_home():
+        for n in range(3):
+            either(stays, home_keep(n).start, home_copy(n).start)
+
+    def send_halo(g):
         for i in range(2):
             halo(i, g, 0).start()
             pl.when(jnp.logical_not(last_chip))(halo(i, g, 1).start)
@@ -264,6 +320,10 @@
         for i in range(2):
             swap(i, g).start()
 
+    send_halo(0)
+    pl.when(sz <= z)(send_home)
+    send_halo(1)
+
     def tot_copy(to):
         return remote(
             tot_out.at[to // 2], tot_in.at[me], tot_send.at[0], tot_recv.at[0], plane_device(to)
@@ -284,9 +344,8 @@
         return pl.ds(q * WIDE, WIDE)
 
     def z_copy(q):
-        return remote(
-            att.at[part(q)], z_in.at[long_out, part(q)], z_send.at[q], z_recv.at[long_out, q], z_to
-        )
+        slot, to = (long_out, z_to) if q < 2 else (half_out, half_to)
+        return remote(att.at[part(q)], z_in.at[slot, part(q)], z_send.at[q], z_recv.at[slot, q], to)
 
     def z_keep(q):
         return pltpu.make_async_copy(att.at[part(q)], z_in.at[0, part(q)], z_recv.at[0, q])
@@ -307,10 +366,6 @@
     def p_keep(q):
         return pltpu.make_async_copy(z_in.at[0, part(q)], att_in.at[part(q)], att_recv.at[q])
 
-    def either(here, keep, leave):
-        pl.when(here)(keep)
-        pl.when(jnp.logical_not(here))(leave)
-
     def sqz_copy():
         return remote(sq_out, sq_mid.at[long_out], sqz_send.at[0], sqz_recv.at[long_out], z_to)
 
@@ -331,16 +386,6 @@
 
     def sq_keep():
         return pltpu.make_async_copy(sq_mid.at[0], sq_in.at[hg], sq_recv.at[hg])
-
-    home_pairs = ((b_v, b_here), (w_out, w_here), (tot_out, tot_here))
-
-    def home_copy(n):
-        return remote(
-            home_pairs[n][0], home_pairs[n][1], home_send.at[n], home_recv.at[n], away
-        )
-
-    def home_keep(n):
-        return pltpu.make_async_copy(home_pairs[n][0], home_pairs[n][1], home_recv.at[n])
 
     def here_copy(r):
         return remote(
@@ -351,6 +396,11 @@
     def here_arrival(r):
         n = (hg + r) % NH
         return remote(sq_here.at[n], sq_here.at[n], here_send.at[r], here_recv.at[n], partner)
+
+    @pl.when(sz > z)
+    def _():
+        pl.semaphore_wait(home_ready, 1)
+        send_home()
 
     sums = [jnp.zeros((1, BLK), F32) for _ in range(2)]
     for g in range(2):
@@ -388,20 +438,22 @@
                 pl.semaphore_wait(ready_sem, 1)
         else:
             sq_out[...] = jnp.broadcast_to(jnp.concatenate(sums, 1), (8, SPAN))
+
+            @pl.when(level < 2)
+            def _():
+                pl.semaphore_wait(head_sem, jnp.where(level == 0, 6, 2))
+
             for r in range(1, NH):
                 here_copy(r).start()
             sq_here[hg] = sq_out[...]
             either(z_stays, lambda: sqz_keep().start(), lambda: sqz_copy().start())
+
+            @pl.when(z < NZ - 1)
+            def _():
+                pl.semaphore_wait(later_sem, NZ - 1 - z)
+
         for q in (2 * g, 2 * g + 1):
             either(z_stays, z_keep(q).start, z_copy(q).start)
-        if g == 0:
-            @pl.when(sz > z)
-            def _():
-                pl.semaphore_wait(home_ready, 1)
-
-            for n in range(3):
-                either(stays, home_keep(n).start, home_copy(n).start)
-
     cross = dot(b_v[...], c_v[...], ((1,), (1,)))
 
     def make_mix(k, carry):
@@ -430,25 +482,27 @@
 
     lax.fori_loop(0, 8, make_ecum, 0)
 
-    @pl.when(jnp.logical_and(relaying, core == 0))
+    @pl.when(jnp.logical_and(jnp.logical_or(relaying, helps), core == 0))
     def _():
         pl.semaphore_wait(ready_sem, 1)
 
-    def arrive(q):
-        @pl.when(relaying)
+    def relay(q):
+        @pl.when(relaying if q < 2 else jnp.logical_or(relaying, helps))
         def _():
             z_arrival(1, q).wait_recv()
             relay_copy(q).start()
 
-        either(z_stays, z_keep(q).wait, z_arrival(0, q).wait_recv)
-        either(p_stays, p_keep(q).start, p_copy(q).start)
-
-    def arrive_squares():
+    def relay_squares():
         @pl.when(relaying)
         def _():
             sqz_arrival(1).wait_recv()
             sqr_copy().start()
 
+    def arrive(q):
+        either(z_stays, z_keep(q).wait, z_arrival(0, q).wait_recv)
+        either(p_stays, p_keep(q).start, p_copy(q).start)
+
+    def arrive_squares():
         either(z_stays, lambda: sqz_keep().wait(), lambda: sqz_arrival(0).wait_recv())
         for r in range(1, NH):
             sq_copy((hg + r) % NH, hg).start()
@@ -465,16 +519,35 @@
             plane_device(to),
         )
 
+    tail = pl.ds(1, 7)
+
     def pre_copy(q, s):
-        return remote(
-            pre_out.at[q, s], pre_in.at[q, z % 2], pre_send.at[q, s], pre_recv.at[q, z % 2],
-            z_device(NZ // 2 * s + z // 2),
+        far = z == (0 if s else NZ - 1)
+        to = jnp.where(far, NZ - 2 if s else 1, NZ // 2 * s + z // 2)
+        slot = jnp.where(far, 2, z % 2)
+        return remote(
+            pre_out.at[q, s, tail], pre_in.at[q, slot, tail], pre_send.at[q, s],
+            pre_recv.at[q, slot], z_device(to),
         )
 
     def pre_arrival(q, n):
-        return remote(
-            pre_in.at[q, n], pre_in.at[q, n], pre_send.at[q, 0], pre_recv.at[q, n], partner
-        )
+        part = pre_in.at[q, n, tail]
+        return remote(part, part, pre_send.at[q, 0], pre_recv.at[q, n], partner)
+
+    pre_relays = jnp.logical_or(z == 1, z == NZ - 2)
+
+    def pre_pass(q):
+        slot = jnp.where(z == 1, 1, 0)
+        return remote(
+            pre_in.at[q, 2, tail], pre_in.at[q, slot, tail], pre_on.at[q], pre_recv.at[q, slot],
+            z_device(jnp.where(z == 1, NZ // 2 - 1, NZ // 2)),
+        )
+
+    def pre_relay(q):
+        @pl.when(pre_relays)
+        def _():
+            pre_arrival(q, 2).wait_recv()
+            pre_pass(q).start()
 
     def run_copy(q, s, to):
         return remote(
@@ -591,12 +664,14 @@
             return carried
 
         carried = lax.fori_loop(0, z, gather, jnp.zeros((SLICE, STATE), F32))
-        for n in range(8):
+        en_out[q, 0] = carried.astype(BF16)
+        for n in range(1, 8):
             value = pre_in[q, 0, n].astype(F32) + starts[n, q:q + 1] * carried
             en_out[q, n] = value.astype(BF16)
         arrived(2 * z)
         carried = jnp.exp(plane_out[0])[q:q + 1] * carried + run_in[q, 2 * z].astype(F32)
-        for n in range(8):
+        en_out[q, 8] = carried.astype(BF16)
+        for n in range(1, 8):
             value = pre_in[q, 1, n].astype(F32) + starts[8 + n, q:q + 1] * carried
             en_out[q, 8 + n] = value.astype(BF16)
         ring(lambda to: en_copy(q, to).start())
@@ -608,6 +683,7 @@
         entry = dot(c_v[...], en_in[q].reshape(HALF, STATE), ((1,), (1,)))
         out_ref[:, lanes] = (local[:, lanes] + ecum[:, lanes] * entry).astype(BF16)
 
+    relay(0)
     for n in range(3):
         either(stays, home_keep(n).wait, home_copy(n).wait_recv)
     ring(lambda to: vtot_copy(to).start())
@@ -617,6 +693,8 @@
     for q in range(HALVES):
         states(q)
 
+    relay(1)
+    relay_squares()
     sent(tot_in, tot_recv.at[0]).wait_recv()
     for r in range(2):
         logs = jnp.zeros((8, 128), F32)
@@ -625,20 +703,20 @@
             logs = logs + tot_in[n]
         plane_out[r] = logs
 
-    @pl.when(z < NZ - 1)
-    def _():
-        pl.semaphore_wait(later_sem, NZ - 1 - z)
-
     each(z + 1, NZ, lambda to: log_copy(to, z).start())
     arrive(0)
+    relay(2)
+    arrive(1)
+    arrive_squares()
     sent(run_tot, vtot_recv.at[0]).wait_recv()
     prefix(0)
     prefix(1)
-    arrive(1)
-    arrive_squares()
+    relay(3)
     arrive(2)
+    arrive(3)
+    pre_relay(0)
+    pre_relay(1)
     locals_(0)
-    arrive(3)
     enter(0)
     enter(1)
     locals_(1)
@@ -663,7 +741,12 @@
     @pl.when(relaying)
     def _():
         sqr_copy().wait_send()
-        for q in range(CHUNKS):
+        for q in range(2):
+            relay_copy(q).wait_send()
+
+    @pl.when(jnp.logical_or(relaying, helps))
+    def _():
+        for q in range(2, CHUNKS):
             relay_copy(q).wait_send()
 
     @pl.when(p_moves)
@@ -688,6 +771,7 @@
         for s in range(2):
             run_targets(s, lambda to: run_copy(q, s, to).wait_send())
             pl.when(NZ // 2 * s + z // 2 != z)(pre_copy(q, s).wait_send)
+        pl.when(pre_relays)(pre_pass(q).wait_send)
         sent(en_out.at[q], en_send.at[q]).wait_send()
 
 
@@ -734,7 +818,7 @@
         vm((HALVES, PLANE, SLICE, STATE), BF16),
         vm((HALVES, PLANE, SLICE, STATE), BF16),
         vm((HALVES, 2, 8, SLICE, STATE), BF16),
-        vm((HALVES, 2, 8, SLICE, STATE), BF16),
+        vm((HALVES, 3, 8, SLICE, STATE), BF16),
         vm((HALVES, 2, SLICE, STATE), BF16),
         vm((HALVES, 2 * NZ, SLICE, STATE), BF16),
         vm((HALVES, PLANE, SLICE, STATE), BF16),
@@ -751,12 +835,13 @@
         dma((NH,)), dma((NH,)),
         dma((3,)), dma((3,)),
         dma((1,)), dma((1,)),
-        dma((HALVES, 2)), dma((HALVES, 2)),
+        dma((HALVES, 2)), dma((HALVES, 3)), dma((HALVES,)),
         dma((1,)), dma((1,)),
         dma((NZ,)), dma((NZ,)),
         dma((HALVES,)), dma((HALVES,)),
         dma((HALVES, 2, NZ)), dma((HALVES, 2 * NZ)),
         dma((HALVES,)), dma((HALVES,)),
+        pltpu.SemaphoreType.REGULAR,
         pltpu.SemaphoreType.REGULAR,
         pltpu.SemaphoreType.REGULAR,
         pltpu.SemaphoreType.REGULAR,

time: 79.9 us -> 60.5 us (0.76)
  the two profiles are of different devices: /device:TPU:193 before, /device:TPU:145 now
where the time goes in v5:
time: 60.5 us; the launch traced here: 60.3 us
  Pallas kernels  58.4 us (97%)
  local copies, waits for them, and re-layouts  1.87 us (3%)
    pallas_call x1, Pallas kernels, body(): pl.pallas_call(kernel, out_shape=jax.ShapeDtypeStruct((SPAN, feats), BF16...  58.4 us
    unnamed x1, local copies, waits for them, and re-layouts  1.87 us

profile of v5, /device:TPU:145, one launch (start us, length us, event | category | flops | bytes accessed | tf_op | source)
XLA Modules:
  0.0 60.3 jit_solution(5158440186908289156)
XLA Ops:
  0.0 58.4 %shard_map.91 = bf16[256,1024]{1,0:T(8,128)(2,1)} custom-call(bf16[2,128,1024]{2,1,0:T(8,128)(2,1)} %q_hbm.1, bf16[2,128,256]{2,1,0:T(8,128)(2,1)} %k_hbm.1, bf16[2,128,256]{2,1,0:T(8,128)(2,1)} %v_hbm.1, f32[8,128]{1,0:T(8,128)} %bitcast.1, bf16[256,128]{1,0:T(8,128)(2,1)} %b_hbm.1, bf16[256,128]{1,0:T(8,128)(2,1)} %c_hbm.1, f32[16,256]{1,0:T(8,128)} %step_hbm.1, ...), custom_call_target="tpu_custom_call" | custom-call | tf_op jit(solution)/shard_map/pallas_call | solution.py:850
  58.4 1.9 %copy.11 = bf16[256,1024]{1,0:T(8,128)(2,1)} copy(bf16[256,1024]{1,0:T(8,128)(2,1)} %shard_map.91) | data formatting | bytes 1048576

commit v6 on v5

--- a/solution.py
+++ b/solution.py
@@ -42,13 +42,13 @@
 
 
 def kernel(
-    q_hbm, k_hbm, v_hbm, gain_hbm, b_hbm, c_hbm, step_hbm, decay_hbm, skip_ref,
+    q_hbm, k_hbm, v_hbm, gain_hbm, b_hbm, c_hbm, step_hbm, decay_hbm, skip_hbm,
     out_ref,
     q_span, k_stage, v_stage, k_win, v_win, gain_v, b_v, c_v, step_v, decay_v,
     cum_v, v_v, gcol, mix, ecum, att, z_in, att_in, sq_out, sq_mid, sq_in, sq_here, weighted, local,
-    w_out, w_here, b_here, tot_here, tot_out, tot_in, run_tot, starts, plane_out, plane_in,
+    w_low, w_here, b_here, tot_low, tot_row, tot_here, tot_out, tot_in, run_tot, starts, plane_out, plane_in,
     st_out, st_in, pre_out, pre_in, run_out, run_in, en_out, en_in,
-    load_sem, halo_send, halo_recv, swap_send, swap_recv, q_send, q_recv, z_send, z_recv,
+    skip_ref, load_sem, halo_send, halo_recv, swap_send, swap_recv, q_send, q_recv, z_send, z_recv,
     relay_send, att_send, att_recv, sqz_send, sqz_recv, sqr_send, sq_send, sq_recv,
     here_send, here_recv, home_send, home_recv, vtot_send, vtot_recv, pre_send, pre_recv, pre_on,
     tot_send, tot_recv, log_send, log_recv, st_send, st_recv, run_send, run_recv,
@@ -112,7 +112,7 @@
         (decay_hbm, decay_v), (step_hbm, step_v), (k_hbm, k_stage), (v_hbm, v_stage),
         (k_hbm.at[core], k_win.at[mine]), (v_hbm.at[core], v_win.at[mine]),
         (q_hbm.at[core], q_span.at[core]),
-        (b_hbm, b_v), (c_hbm, c_v), (gain_hbm, gain_v),
+        (b_hbm, b_v), (c_hbm, c_v), (gain_hbm, gain_v), (skip_hbm, skip_ref),
     ]
     loads = [pltpu.make_async_copy(s, d, load_sem.at[i]) for i, (s, d) in enumerate(loads)]
     for copy in loads:
@@ -201,7 +201,9 @@
     causal = row <= col
     cum = dot(decay_v[...], causal.astype(F32), ((1,), (0,)), precision=lax.Precision.HIGHEST)
     total = cum[:, SPAN - 1:]
-    w_out[...] = jnp.exp(total - cum) * step_v[...]
+    tail_weight = jnp.exp(total - cum) * step_v[...]
+    w_low[...] = tail_weight.astype(BF16)
+    tot_low[...] = jnp.broadcast_to(total, (16, 128))
     shift = jnp.log(step_v[...]) - cum
     for k in range(16):
         cum_v[k] = jnp.broadcast_to(cum[k:k + 1], (8, SPAN))
@@ -298,7 +300,7 @@
         return remote(part, part, q_send.at[g], q_recv.at[g], partner)
 
     last_chip = chip == CHIPS - 1
-    home_pairs = ((b_v, b_here), (w_out, w_here), (tot_out, tot_here))
+    home_pairs = ((b_v, b_here), (w_low, w_here), (tot_low, tot_row))
 
     def home_copy(n):
         return remote(
@@ -519,19 +521,19 @@
             plane_device(to),
         )
 
-    tail = pl.ds(1, 7)
+    after_first = pl.ds(1, 7)
 
     def pre_copy(q, s):
         far = z == (0 if s else NZ - 1)
         to = jnp.where(far, NZ - 2 if s else 1, NZ // 2 * s + z // 2)
         slot = jnp.where(far, 2, z % 2)
         return remote(
-            pre_out.at[q, s, tail], pre_in.at[q, slot, tail], pre_send.at[q, s],
+            pre_out.at[q, s, after_first], pre_in.at[q, slot, after_first], pre_send.at[q, s],
             pre_recv.at[q, slot], z_device(to),
         )
 
     def pre_arrival(q, n):
-        part = pre_in.at[q, n, tail]
+        part = pre_in.at[q, n, after_first]
         return remote(part, part, pre_send.at[q, 0], pre_recv.at[q, n], partner)
 
     pre_relays = jnp.logical_or(z == 1, z == NZ - 2)
@@ -539,7 +541,7 @@
     def pre_pass(q):
         slot = jnp.where(z == 1, 1, 0)
         return remote(
-            pre_in.at[q, 2, tail], pre_in.at[q, slot, tail], pre_on.at[q], pre_recv.at[q, slot],
+            pre_in.at[q, 2, after_first], pre_in.at[q, slot, after_first], pre_on.at[q], pre_recv.at[q, slot],
             z_device(jnp.where(z == 1, NZ // 2 - 1, NZ // 2)),
         )
 
@@ -590,7 +592,7 @@
             gain = gcol[rows, :]
             value = att[rows, :].astype(F32) * jnp.concatenate([gain, gain], 1) * rate
             value = value.astype(BF16).astype(F32)
-            weighted[rows, :] = (value * w_here[k:k + 1, :]).astype(BF16)
+            weighted[rows, :] = (value * w_here[k:k + 1, :].astype(F32)).astype(BF16)
         state = dot(weighted[q * HALF:(q + 1) * HALF], b_here[...], ((1,), (0,)))
         st_out[q] = state.astype(BF16).reshape(PLANE, SLICE, STATE)
         ring(lambda to: st_copy(q, to).start())
@@ -686,6 +688,9 @@
     relay(0)
     for n in range(3):
         either(stays, home_keep(n).wait, home_copy(n).wait_recv)
+    for o in range(8):
+        lines = [tot_row[8 * (n % 2) + o:8 * (n % 2) + o + 1] for n in range(8)]
+        tot_here[o] = jnp.concatenate(lines, 0)
     ring(lambda to: vtot_copy(to).start())
     run_tot[me] = tot_here[me // 2]
     for r in range(1, NH):
@@ -805,9 +810,11 @@
         vm((NH, 8, SPAN), F32),
         vm((feats, SPAN), BF16),
         vm((SPAN, feats), F32),
-        vm((16, SPAN), F32),
-        vm((16, SPAN), F32),
+        vm((16, SPAN), BF16),
+        vm((16, SPAN), BF16),
         vm((SPAN, STATE), BF16),
+        vm((16, 128), F32),
+        vm((16, 128), F32),
         vm((8, 8, 128), F32),
         vm((8, 8, 128), F32),
         vm((PLANE, 8, 128), F32),
@@ -823,7 +830,8 @@
         vm((HALVES, 2 * NZ, SLICE, STATE), BF16),
         vm((HALVES, PLANE, SLICE, STATE), BF16),
         vm((HALVES, PLANE, SLICE, STATE), BF16),
-        dma((10,)),
+        pltpu.SMEM((16,), F32),
+        dma((11,)),
         dma((2, 2, 2)), dma((2, 2, 2)),
         dma((2, 2)), dma((2, 2)),
         dma((2,)), dma((2,)),
@@ -846,15 +854,21 @@
         pltpu.SemaphoreType.REGULAR,
         pltpu.SemaphoreType.REGULAR,
     ]
-    anywhere = pl.BlockSpec(memory_space=pl.ANY)
+    anywhere = pl.BlockSpec(memory_space=pltpu.HBM)
+    pinned = [
+        pltpu.with_memory_space_constraint(a, pltpu.HBM)
+        for a in (query, keys, values, gain, in_b, out_c, step, log_decay, skip)
+    ]
     return pl.pallas_call(
         kernel,
         out_shape=jax.ShapeDtypeStruct((SPAN, feats), BF16),
-        in_specs=[anywhere] * 8 + [pl.BlockSpec(memory_space=pltpu.SMEM)],
+        in_specs=[anywhere] * 9,
         out_specs=pl.BlockSpec(memory_space=pltpu.VMEM),
         scratch_shapes=scratch,
-        compiler_params=pltpu.CompilerParams(collective_id=0, has_side_effects=True),
-    )(query, keys, values, gain, in_b, out_c, step, log_decay, skip)
+        compiler_params=pltpu.CompilerParams(
+            collective_id=0, has_side_effects=True, vmem_limit_bytes=24 * 1024 * 1024
+        ),
+    )(*pinned)
 
 
 def solution(mesh):

time: 60.5 us -> 56.1 us (0.927)
  the two profiles are of different devices: /device:TPU:145 before, /device:TPU:113 now
where the time goes in v6:
time: 56.1 us; the launch traced here: 56 us
  Pallas kernels  55.2 us (98%)
  local copies, waits for them, and re-layouts  0.8 us (1%)
    pallas_call x1, Pallas kernels, body(): pl.pallas_call(kernel, out_shape=jax.ShapeDtypeStruct((SPAN, feats), BF16...  55.2 us

profile of v6, /device:TPU:113, one launch (start us, length us, event | category | flops | bytes accessed | tf_op | source)
XLA Modules:
  0.0 56.0 jit_solution(4270845190154266025)
XLA Ops:
  0.0 55.2 %shard_map.91 = bf16[256,1024]{1,0:T(8,128)(2,1)S(1)} custom-call(bf16[2,128,1024]{2,1,0:T(8,128)(2,1)} %q_hbm.1, bf16[2,128,256]{2,1,0:T(8,128)(2,1)} %k_hbm.1, bf16[2,128,256]{2,1,0:T(8,128)(2,1)} %v_hbm.1, f32[8,128]{1,0:T(8,128)} %bitcast.1, bf16[256,128]{1,0:T(8,128)(2,1)} %b_hbm.1, bf16[256,128]{1,0:T(8,128)(2,1)} %c_hbm.1, f32[16,256]{1,0:T(8,128)} %step_hbm.1, ...), custom_call_target="tpu_custom_call" | custom-call | tf_op jit(solution)/shard_map/pallas_call | solution.py:862
  55.2 0.8 %copy.11 = bf16[256,1024]{1,0:T(8,128)(2,1)} copy(bf16[256,1024]{1,0:T(8,128)(2,1)S(1)} %shard_map.91) | data formatting | bytes 1048576

commit v7 on v6

--- a/solution.py
+++ b/solution.py
@@ -488,8 +488,8 @@
     def _():
         pl.semaphore_wait(ready_sem, 1)
 
-    def relay(q):
-        @pl.when(relaying if q < 2 else jnp.logical_or(relaying, helps))
+    def relay(q, here):
+        @pl.when(here)
         def _():
             z_arrival(1, q).wait_recv()
             relay_copy(q).start()
@@ -685,7 +685,7 @@
         entry = dot(c_v[...], en_in[q].reshape(HALF, STATE), ((1,), (1,)))
         out_ref[:, lanes] = (local[:, lanes] + ecum[:, lanes] * entry).astype(BF16)
 
-    relay(0)
+    relay(0, relaying)
     for n in range(3):
         either(stays, home_keep(n).wait, home_copy(n).wait_recv)
     for o in range(8):
@@ -698,7 +698,7 @@
     for q in range(HALVES):
         states(q)
 
-    relay(1)
+    relay(1, relaying)
     relay_squares()
     sent(tot_in, tot_recv.at[0]).wait_recv()
     for r in range(2):
@@ -709,21 +709,29 @@
         plane_out[r] = logs
 
     each(z + 1, NZ, lambda to: log_copy(to, z).start())
-    arrive(0)
-    relay(2)
-    arrive(1)
-    arrive_squares()
+    late = jnp.logical_or(
+        jnp.logical_and(core == 0, z // 2 == 2), jnp.logical_and(core == 1, z // 2 == 1)
+    )
+    prompt = jnp.logical_not(late)
+    pl.when(prompt)(lambda: arrive(0))
+    relay(2, relaying)
+    pl.when(prompt)(lambda: arrive(1))
+    relay(3, relaying)
     sent(run_tot, vtot_recv.at[0]).wait_recv()
     prefix(0)
     prefix(1)
-    relay(3)
+    relay(2, helps)
+    relay(3, helps)
+    for q in range(2):
+        pl.when(late)(lambda: arrive(q))
+    arrive_squares()
     arrive(2)
     arrive(3)
     pre_relay(0)
     pre_relay(1)
-    locals_(0)
     enter(0)
     enter(1)
+    locals_(0)
     locals_(1)
     finish(0)
     finish(1)

time: 56.1 us -> 52.6 us (0.938)
  the two profiles are of different devices: /device:TPU:113 before, /device:TPU:148 now
where the time goes in v7:
time: 52.6 us; the launch traced here: 52.4 us
  Pallas kernels  51.6 us (98%)
  local copies, waits for them, and re-layouts  0.8 us (2%)
    pallas_call x1, Pallas kernels, body(): pl.pallas_call(kernel, out_shape=jax.ShapeDtypeStruct((SPAN, feats), BF16...  51.6 us

profile of v7, /device:TPU:148, one launch (start us, length us, event | category | flops | bytes accessed | tf_op | source)
XLA Modules:
  0.0 52.4 jit_solution(6074891245467586790)
XLA Ops:
  0.0 51.6 %shard_map.91 = bf16[256,1024]{1,0:T(8,128)(2,1)S(1)} custom-call(bf16[2,128,1024]{2,1,0:T(8,128)(2,1)} %q_hbm.1, bf16[2,128,256]{2,1,0:T(8,128)(2,1)} %k_hbm.1, bf16[2,128,256]{2,1,0:T(8,128)(2,1)} %v_hbm.1, f32[8,128]{1,0:T(8,128)} %bitcast.1, bf16[256,128]{1,0:T(8,128)(2,1)} %b_hbm.1, bf16[256,128]{1,0:T(8,128)(2,1)} %c_hbm.1, f32[16,256]{1,0:T(8,128)} %step_hbm.1, ...), custom_call_target="tpu_custom_call" | custom-call | tf_op jit(solution)/shard_map/pallas_call | solution.py:870
  51.6 0.8 %copy.11 = bf16[256,1024]{1,0:T(8,128)(2,1)} copy(bf16[256,1024]{1,0:T(8,128)(2,1)S(1)} %shard_map.91) | data formatting | bytes 1048576

commit v8 on v7

--- a/solution.py
+++ b/solution.py
@@ -105,6 +105,82 @@
     away = (sz, sx, sy, seq // CHIPS, hg)
     stays = span == seq
 
+    barrier = pltpu.get_barrier_semaphore()
+
+    def greet(device):
+        pl.semaphore_signal(barrier, inc=1, device_id=device, device_id_type=MESH)
+
+    def plane_device(index):
+        return (z, index // (NY * NC), (index // NC) % NY, index % NC, hg)
+
+    def z_device(index):
+        return (index, x, y, core, hg)
+
+    def ring(act):
+        def visit(r, carry):
+            act((me + r) % PLANE)
+            return carry
+
+        lax.fori_loop(1, PLANE, visit, 0)
+
+    def each(low, high, act):
+        def visit(n, carry):
+            act(n)
+            return carry
+
+        lax.fori_loop(low, high, visit, 0)
+
+    greet((bz, bx, by, 0, hg))
+    greet((bz, bx, by, 1, hg))
+    ring(lambda n: greet(plane_device(n)))
+
+    def rank(h):
+        return jnp.where(h == 0, 0, jnp.where(h == 2, 2, 1))
+
+    level = rank(hg)
+    same = (z, x, y, core)
+
+    def to_heads(position, test, act):
+        for r in range(1, NH):
+            h = (hg + r) % NH
+
+            @pl.when(test(rank(h)))
+            def _():
+                act((*position, h))
+
+    to_heads(p_from[:4], lambda n: n >= level, greet)
+    to_heads(p_to[:4], lambda n: n > level, greet)
+    to_heads(same, lambda n: n >= level, greet)
+
+    @pl.when(jnp.logical_and(z_moves, from_z > z))
+    def _():
+        greet(z_from)
+
+    @pl.when(jnp.logical_and(z_moves, to_z > z))
+    def _():
+        greet(z_to)
+
+    @pl.when(jnp.logical_and(relaying, core == 0))
+    def _():
+        greet(relay_from)
+
+    @pl.when(jnp.logical_and(jnp.logical_or(relaying, helps), core == 0))
+    def _():
+        greet(relay_to)
+
+    @pl.when(jnp.logical_and(z == 5, core == 0))
+    def _():
+        greet((NZ - 1, x, y, 1, hg))
+
+    each(z + 1, NZ, lambda n: greet(z_device(n)))
+    @pl.when(fz > z)
+    def _():
+        greet(home)
+
+    @pl.when(sz > z)
+    def _():
+        greet(away)
+
     mine = pl.ds(pl.multiple_of((2 + core) * BLK, BLK), BLK)
     theirs = pl.ds(pl.multiple_of((2 + other) * BLK, BLK), BLK)
     prev_row = pl.ds(pl.multiple_of(core * BLK, BLK), BLK)
@@ -117,82 +193,6 @@
     loads = [pltpu.make_async_copy(s, d, load_sem.at[i]) for i, (s, d) in enumerate(loads)]
     for copy in loads:
         copy.start()
-
-    barrier = pltpu.get_barrier_semaphore()
-
-    def greet(device):
-        pl.semaphore_signal(barrier, inc=1, device_id=device, device_id_type=MESH)
-
-    def plane_device(index):
-        return (z, index // (NY * NC), (index // NC) % NY, index % NC, hg)
-
-    def z_device(index):
-        return (index, x, y, core, hg)
-
-    def ring(act):
-        def visit(r, carry):
-            act((me + r) % PLANE)
-            return carry
-
-        lax.fori_loop(1, PLANE, visit, 0)
-
-    def each(low, high, act):
-        def visit(n, carry):
-            act(n)
-            return carry
-
-        lax.fori_loop(low, high, visit, 0)
-
-    greet((bz, bx, by, 0, hg))
-    greet((bz, bx, by, 1, hg))
-    ring(lambda n: greet(plane_device(n)))
-
-    def rank(h):
-        return jnp.where(h == 0, 0, jnp.where(h == 2, 2, 1))
-
-    level = rank(hg)
-    same = (z, x, y, core)
-
-    def to_heads(position, test, act):
-        for r in range(1, NH):
-            h = (hg + r) % NH
-
-            @pl.when(test(rank(h)))
-            def _():
-                act((*position, h))
-
-    to_heads(p_from[:4], lambda n: n >= level, greet)
-    to_heads(p_to[:4], lambda n: n > level, greet)
-    to_heads(same, lambda n: n >= level, greet)
-
-    @pl.when(jnp.logical_and(z_moves, from_z > z))
-    def _():
-        greet(z_from)
-
-    @pl.when(jnp.logical_and(z_moves, to_z > z))
-    def _():
-        greet(z_to)
-
-    @pl.when(jnp.logical_and(relaying, core == 0))
-    def _():
-        greet(relay_from)
-
-    @pl.when(jnp.logical_and(jnp.logical_or(relaying, helps), core == 0))
-    def _():
-        greet(relay_to)
-
-    @pl.when(jnp.logical_and(z == 5, core == 0))
-    def _():
-        greet((NZ - 1, x, y, 1, hg))
-
-    each(z + 1, NZ, lambda n: greet(z_device(n)))
-    @pl.when(fz > z)
-    def _():
-        greet(home)
-
-    @pl.when(sz > z)
-    def _():
-        greet(away)
 
     loads[0].wait()
     loads[1].wait()
@@ -338,9 +338,11 @@
         gcol[p * BLK:(p + 1) * BLK, :] = jnp.transpose(line)
 
     scale = math.log2(math.e) / math.sqrt(HDIM)
-    j = lax.broadcasted_iota(jnp.int32, (3 * BLK, 4 * BLK), 0)
-    i = lax.broadcasted_iota(jnp.int32, (3 * BLK, 4 * BLK), 1) % BLK
+    j = lax.broadcasted_iota(jnp.int32, (BLK, 4 * BLK), 0)
+    i = lax.broadcasted_iota(jnp.int32, (BLK, 4 * BLK), 1) % BLK
     first = one(span == 0)
+    recent = j > i + first * BLK
+    until = j <= i
 
     def part(q):
         return pl.ds(q * WIDE, WIDE)
@@ -421,9 +423,13 @@
             vals = jnp.transpose(v_win[a * BLK:(a + 3) * BLK, lanes])
             heads = [q_span[a, :, (4 * g + h) * HDIM:(4 * g + h + 1) * HDIM] for h in range(4)]
             score = dot(keys, jnp.concatenate(heads, 0), ((1,), (1,)))
-            low = jnp.maximum(i + 1, first * (2 - a) * BLK)
-            allowed = (j >= low) & (j <= i + 2 * BLK)
-            score = jnp.where(allowed, score, -jnp.inf)
+            middle = score[BLK:2 * BLK]
+            if a == 0:
+                middle = jnp.where(first == 1, -jnp.inf, middle)
+            score = jnp.concatenate([
+                jnp.where(recent, score[:BLK], -jnp.inf), middle,
+                jnp.where(until, score[2 * BLK:], -jnp.inf),
+            ], 0)
             peak = jnp.max(score, axis=0, keepdims=True)
             terms = jnp.exp2((score - peak) * scale)
             sum_terms = jnp.sum(terms, axis=0, keepdims=True)
@@ -717,10 +723,11 @@
     relay(2, relaying)
     pl.when(prompt)(lambda: arrive(1))
     relay(3, relaying)
+    relay(2, jnp.logical_and(helps, z == 0))
     sent(run_tot, vtot_recv.at[0]).wait_recv()
     prefix(0)
     prefix(1)
-    relay(2, helps)
+    relay(2, jnp.logical_and(helps, z > 0))
     relay(3, helps)
     for q in range(2):
         pl.when(late)(lambda: arrive(q))
@@ -732,8 +739,8 @@
     enter(0)
     enter(1)
     locals_(0)
+    finish(0)
     locals_(1)
-    finish(0)
     finish(1)
 
     for g in range(2):

time: 52.6 us -> 52.4 us (level)
  the two profiles are of different devices: /device:TPU:148 before, /device:TPU:149 now
where the time goes in v8:
time: 52.4 us; the launch traced here: 52.2 us
  Pallas kernels  51.4 us (98%)
  local copies, waits for them, and re-layouts  0.8 us (2%)
    pallas_call x1, Pallas kernels, body(): pl.pallas_call(kernel, out_shape=jax.ShapeDtypeStruct((SPAN, feats), BF16...  51.4 us

profile of v8, /device:TPU:149, one launch (start us, length us, event | category | flops | bytes accessed | tf_op | source)
XLA Modules:
  0.0 52.2 jit_solution(3991267843758332264)
XLA Ops:
  0.0 51.4 %shard_map.91 = bf16[256,1024]{1,0:T(8,128)(2,1)S(1)} custom-call(bf16[2,128,1024]{2,1,0:T(8,128)(2,1)} %q_hbm.1, bf16[2,128,256]{2,1,0:T(8,128)(2,1)} %k_hbm.1, bf16[2,128,256]{2,1,0:T(8,128)(2,1)} %v_hbm.1, f32[8,128]{1,0:T(8,128)} %bitcast.1, bf16[256,128]{1,0:T(8,128)(2,1)} %b_hbm.1, bf16[256,128]{1,0:T(8,128)(2,1)} %c_hbm.1, f32[16,256]{1,0:T(8,128)} %step_hbm.1, ...), custom_call_target="tpu_custom_call" | custom-call | tf_op jit(solution)/shard_map/pallas_call | solution.py:877
  51.4 0.8 %copy.11 = bf16[256,1024]{1,0:T(8,128)(2,1)} copy(bf16[256,1024]{1,0:T(8,128)(2,1)S(1)} %shard_map.91) | data formatting | bytes 1048576

commit v9 on v8

--- a/solution.py
+++ b/solution.py
@@ -724,11 +724,12 @@
     pl.when(prompt)(lambda: arrive(1))
     relay(3, relaying)
     relay(2, jnp.logical_and(helps, z == 0))
+    relay(3, jnp.logical_and(helps, z == 0))
     sent(run_tot, vtot_recv.at[0]).wait_recv()
     prefix(0)
     prefix(1)
     relay(2, jnp.logical_and(helps, z > 0))
-    relay(3, helps)
+    relay(3, jnp.logical_and(helps, z > 0))
     for q in range(2):
         pl.when(late)(lambda: arrive(q))
     arrive_squares()

time: 52.4 us -> 53.1 us (1.013)
  the two profiles are of different devices: /device:TPU:149 before, /device:TPU:191 now
where the time goes in v9:
time: 53.1 us; the launch traced here: 52.9 us
  Pallas kernels  52.1 us (98%)
  local copies, waits for them, and re-layouts  0.8 us (2%)
    pallas_call x1, Pallas kernels, body(): pl.pallas_call(kernel, out_shape=jax.ShapeDtypeStruct((SPAN, feats), BF16...  52.1 us

profile of v9, /device:TPU:191, one launch (start us, length us, event | category | flops | bytes accessed | tf_op | source)
XLA Modules:
  0.0 52.9 jit_solution(18368853045936582436)
XLA Ops:
  0.0 52.1 %shard_map.91 = bf16[256,1024]{1,0:T(8,128)(2,1)S(1)} custom-call(bf16[2,128,1024]{2,1,0:T(8,128)(2,1)} %q_hbm.1, bf16[2,128,256]{2,1,0:T(8,128)(2,1)} %k_hbm.1, bf16[2,128,256]{2,1,0:T(8,128)(2,1)} %v_hbm.1, f32[8,128]{1,0:T(8,128)} %bitcast.1, bf16[256,128]{1,0:T(8,128)(2,1)} %b_hbm.1, bf16[256,128]{1,0:T(8,128)(2,1)} %c_hbm.1, f32[16,256]{1,0:T(8,128)} %step_hbm.1, ...), custom_call_target="tpu_custom_call" | custom-call | tf_op jit(solution)/shard_map/pallas_call | solution.py:878
  52.1 0.8 %copy.11 = bf16[256,1024]{1,0:T(8,128)(2,1)} copy(bf16[256,1024]{1,0:T(8,128)(2,1)S(1)} %shard_map.91) | data formatting | bytes 1048576
